TPU v7x, 256 devices: a 8x8x2 block of a 8x8x16 slice. The times are simulated.
256 devices in a mesh: groups: 2 (over z), tensor: 64 (over x, y), seq: 2 (over core).
Axes of the slice: x: 8, y: 8, z: 2, core: 2. Of those that a mesh axis runs over, the one named last changes fastest.
The devices are a block of a 8x8x16 slice.
Arguments:
- heads_out: bfloat16 [1024, 4096], P(('groups', 'seq'), 'tensor'), parts along dimension 0, may hold values from -6 to 6
- stream_in: bfloat16 [1024, 8192], P(('groups', 'seq', 'tensor')), parts along dimension 0, may hold values from -40 to 40, as said below
- proj_levels: bfloat16 [4096, 8192], P('tensor'), may hold values from -8 to 7, as said below
- proj_scale: float32 [8192], replicated, may hold values from 0.001703125 to 0.006796875
- norm_gain: float32 [8192], replicated, may hold values from 0.25 to 1.75
- gate_levels: bfloat16 [8192, 14336], P(None, 'tensor'), may hold values from -8 to 7, as said below
- gate_scale: float32 [14336], P('tensor'), may hold values from 0.0012153398 to 0.004861359
- gate_index: int32 [64, 8], P('tensor'), may hold values from 0 to 223, as said below
- gate_extra: bfloat16 [8192, 512], P(None, 'tensor'), may hold values from -0.29882812 to 0.29882812
- up_levels: bfloat16 [8192, 14336], P(None, 'tensor'), may hold values from -8 to 7, as said below
- up_scale: float32 [14336], P('tensor'), may hold values from 0.0012153398 to 0.004861359
- up_index: int32 [64, 8], P('tensor'), may hold values from 0 to 223, as said below
- up_extra: bfloat16 [8192, 512], P(None, 'tensor'), may hold values from -0.29882812 to 0.29882812
- down_levels: bfloat16 [14336, 8192], P('tensor'), may hold values from -8 to 7, as said below
- down_scale: float32 [8192], replicated, may hold values from 0.0009020067 to 0.003591323
- down_index: int32 [64, 8], P('tensor'), may hold values from 0 to 8191, as said below
- down_extra: bfloat16 [14336, 8], P('tensor'), may hold values from -0.29882812 to 0.29882812
Outputs:
- stream_out: bfloat16 [1024, 8192], P(('groups', 'seq', 'tensor')), parts along dimension 0
There are 2 independent parts, one for each index of `groups`. A program takes and returns all parts, laid end to end along the dimension named above; an argument that names none is the same for every part. Nothing has to cross between parts.
Inputs may be any that keep to these rules, and one draw needn't show every extreme that they name: stream_in has rows and columns of differing scales. `proj_levels`: integer values. `gate_levels`: integer values. `up_levels`: integer values. `down_levels`: integer values. `gate_index`: each row holds 8 different numbers. `up_index`: each row holds 8 different numbers. `down_index`: each row holds 8 different numbers.
All inputs are finite; a program needn't handle non-finite values.
Results may differ from a plain program's by a relative error of at most 0.0055.
Values may be sent and summed in bfloat16 or wider, within the bound.
A program may use at most 128 MiB of HBM per device.

v0:
```python
import jax
import jax.numpy as jnp
from jax import lax
from jax.sharding import Mesh
from jax.sharding import PartitionSpec as P

TENSOR = ("tensor_0", "tensor_1")
GROUPS_SEQ_TENSOR = ("groups", "seq", "tensor_0", "tensor_1")


def own_rows_2(running, axes):
    for axis in axes:
        running = lax.psum_scatter(running, axis, scatter_dimension=0, tiled=True)
    return running


def rms_norm(mixed, norm_gain):
    mean_sq = jnp.mean(mixed * mixed, axis=-1, keepdims=True)
    return (mixed * lax.rsqrt(mean_sq + 1e-05) * norm_gain).astype(jnp.bfloat16)


def picker(index_row, width):
    return (index_row[:, None] == jnp.arange(width, dtype=jnp.int32)[None, :]).astype(jnp.float32)


def project(rows_in, levels, scale, extra, chosen):
    base = jnp.dot(rows_in, levels, preferred_element_type=jnp.float32)
    added = jnp.dot(rows_in, extra, preferred_element_type=jnp.float32)
    return base * scale + jnp.dot(added, chosen, precision=lax.Precision.HIGHEST)


def local(
    heads_out,
    stream_in,
    proj_levels,
    proj_scale,
    norm_gain,
    gate_levels,
    gate_scale,
    gate_index,
    gate_extra,
    up_levels,
    up_scale,
    up_index,
    up_extra,
    down_levels,
    down_scale,
    down_index,
    down_extra,
):
    shard_width = gate_levels.shape[1]
    model_width = proj_levels.shape[1]
    gate_pick = picker(gate_index[0], shard_width)
    up_pick = picker(up_index[0], shard_width)
    down_pick = picker(down_index[0], model_width)
    taken = heads_out
    proj = own_rows_2(
        jnp.dot(taken, proj_levels, preferred_element_type=jnp.float32) * proj_scale, TENSOR
    )
    mixed = stream_in.astype(jnp.float32) + proj
    normed = rms_norm(mixed, norm_gain)
    normed_rows = lax.all_gather(normed, TENSOR, axis=0, tiled=True)
    gate = project(normed_rows, gate_levels, gate_scale, gate_extra, gate_pick)
    up = project(normed_rows, up_levels, up_scale, up_extra, up_pick)
    hidden = (jax.nn.silu(gate) * up).astype(jnp.bfloat16)
    taken = hidden
    down = own_rows_2(project(taken, down_levels, down_scale, down_extra, down_pick), TENSOR)
    return (mixed + down).astype(jnp.bfloat16)


def solution(mesh):
    torus = Mesh(
        mesh.devices.reshape(mesh.shape["groups"], 8, 8, mesh.shape["seq"]),
        ("groups", "tensor_0", "tensor_1", "seq"),
    )
    return jax.shard_map(
        local,
        mesh=torus,
        in_specs=(
            P(("groups", "seq"), TENSOR),
            P(GROUPS_SEQ_TENSOR, None),
            P(TENSOR, None),
            P(),
            P(),
            P(None, TENSOR),
            P(TENSOR),
            P(TENSOR, None),
            P(None, TENSOR),
            P(None, TENSOR),
            P(TENSOR),
            P(TENSOR, None),
            P(None, TENSOR),
            P(TENSOR, None),
            P(),
            P(TENSOR, None),
            P(TENSOR, None),
        ),
        out_specs=P(GROUPS_SEQ_TENSOR, None),
        check_vma=False,
    )
```

profile of v0, /device:TPU:514, one launch (start us, length us, event | category | flops | bytes accessed | tf_op | source)
XLA Modules:
  0.0 497.5 jit_solution(14102043110908546794)
XLA Ops:
  6.6 1.2 copy-done
  7.8 5.3 %convolution_multiply_fusion.1 = f32[256,8192]{1,0:T(8,128)} fusion(bf16[256,64]{0,1:T(8,128)(2,1)} %param.17, bf16[64,8192]{1,0:T(8,128)(2,1)S(1)} %copy-done, f32[8192]{0:T(1024)} %param.20), kind=kOutput, calls=%fused_computation.2 | convolution fusion | flops 270532608 | bytes 9502720 | tf_op jit(solution)/shard_map/dot_general | solution.py:58
  13.1 0.1 reduce-scatter.3.cloned.1.call-update
  13.1 0.1 all-reduce.5.cloned.1.call-start
  13.2 112.5 %reduce-scatter.3.cloned.1.call-done = f32[32,8192]{1,0:T(8,128)} async-done(((f32[256,8192]{1,0:T(8,128)}), f32[32,8192]{1,0:T(8,128)}) %reduce-scatter.3.cloned.1.call-update) | async-done | bytes 1048592 | tf_op jit(solution)/shard_map/reduce_scatter | solution.py:13
  125.7 0.1 all-reduce.5.cloned.1.call-update
  125.7 0.1 all-gather.3.cloned.1.call-start
  125.8 0.6 dynamic-slice
  127.0 80.4 %all-reduce.5.cloned.1.call-done = f32[32,8192]{1,0:T(8,128)} async-done(((f32[32,8192]{1,0:T(8,128)}), f32[32,8192]{1,0:T(8,128)}) %all-reduce.5.cloned.1.call-update) | async-done | bytes 1048592
  207.4 1.1 multiply_reduce_fusion
  208.6 1.7 fusion.4
  210.3 0.1 all-gather.3.cloned.1.call-update
  210.3 0.0 copy-start.11
  210.3 0.1 reduce-scatter.5.cloned.1.call-start
  210.4 81.7 %all-gather.3.cloned.1.call-done = bf16[64,4,8192]{2,1,0:T(4,128)(2,1)} async-done(((bf16[1,4,8192]{2,1,0:T(4,128)(2,1)}), bf16[64,4,8192]{2,1,0:T(4,128)(2,1)}) %all-gather.3.cloned.1.call-update) | async-done | bytes 4194320 | tf_op jit(solution)/shard_map/all_gather | solution.py:62
  292.1 7.0 %reshape.17 = bf16[256,8192]{1,0:T(8,128)(2,1)} reshape(bf16[64,4,8192]{2,1,0:T(4,128)(2,1)} %all-gather.3.cloned.1.call-done) | data formatting | bytes 8388608
  299.1 3.6 fusion.8
  302.7 1.2 fusion.7
  303.9 1.6 convolution_multiply_fusion.2
  305.5 0.4 copy-done.10
  306.0 1.4 convolution_multiply_fusion.3
  307.4 0.4 convolution_add_fusion.2
  307.8 0.4 fusion.1
  308.1 0.2 fusion.9
  308.4 1.3 convolution_multiply_fusion
  309.7 5.9 %convolution_add_fusion = f32[256,8192]{1,0:T(8,128)} fusion(f32[256,8192]{1,0:T(8,128)S(1)} %convolution_multiply_fusion, f32[256,8]{1,0:T(8,128)S(1)} %fusion.9, s32[8]{0:T(128)S(1)} %bitcast.23), kind=kOutput, calls=%fused_computation | convolution fusion | flops 203489280 | bytes 16785440 | tf_op jit(solution)/shard_map/dot_general | solution.py:29
  315.6 0.1 reduce-scatter.5.cloned.1.call-update
  315.6 0.1 all-reduce.7.cloned.1.call-start
  315.7 91.8 %reduce-scatter.5.cloned.1.call-done = f32[32,8192]{1,0:T(8,128)} async-done(((f32[256,8192]{1,0:T(8,128)}), f32[32,8192]{1,0:T(8,128)}) %reduce-scatter.5.cloned.1.call-update) | async-done | bytes 1048592 | tf_op jit(solution)/shard_map/reduce_scatter | solution.py:13
  407.5 0.1 all-reduce.7.cloned.1.call-update
  407.6 81.7 %all-reduce.7.cloned.1.call-done = f32[32,8192]{1,0:T(8,128)} async-done(((f32[32,8192]{1,0:T(8,128)}), f32[32,8192]{1,0:T(8,128)}) %all-reduce.7.cloned.1.call-update) | async-done | bytes 1048592
  489.2 1.7 fusion.2
  (33 shorter events, 0.1 us)
Async XLA Ops:
  6.5 1.2 copy-start
  6.6 119.1 %reduce-scatter.3.cloned.1.call-start = ((), (), s32[]{:S(2)}) async-start(), calls=%async_computation.2 | async-start | bytes 9437184 | tf_op jit(solution)/shard_map/reduce_scatter | solution.py:13
  13.1 112.7 %copy-start.16 = (u32[256]{0:T(256)S(1)}, u32[256]{0:T(256)}, u32[]{:S(2)}) copy-start(u32[256]{0:T(256)} %constant.24) | copy-start | bytes 3076
  13.1 194.4 %copy-start.3 = (bf16[4,8192]{1,0:T(4,128)(2,1)S(1)}, bf16[4,8192]{1,0:T(4,128)(2,1)}, u32[]{:S(2)}) copy-start(bf16[4,8192]{1,0:T(4,128)(2,1)} %param.18) | copy-start | bytes 196612
  13.1 195.5 %copy-start.5 = (f32[8192]{0:T(1024)S(1)}, f32[8192]{0:T(1024)}, u32[]{:S(2)}) copy-start(f32[8192]{0:T(1024)} %param.21) | copy-start | bytes 98308
  13.1 194.3 %all-reduce.5.cloned.1.call-start = ((), (), s32[]{:S(2)}) async-start(), calls=%async_computation.5 | async-start | bytes 2097152
  125.7 166.3 %all-gather.3.cloned.1.call-start = ((), (), s32[]{:S(2)}) async-start(), calls=%async_computation.4 | async-start | bytes 4259840 | tf_op jit(solution)/shard_map/all_gather | solution.py:62
  210.3 88.7 %copy-start.11 = (bf16[8192,8]{0,1:T(8,128)(2,1)S(1)}, bf16[8192,8]{0,1:T(8,128)(2,1)}, u32[]{:S(2)}) copy-start(bf16[8192,8]{0,1:T(8,128)(2,1)} %param.29) | copy-start | bytes 393220
  210.3 197.2 %reduce-scatter.5.cloned.1.call-start = ((), (), s32[]{:S(2)}) async-start(), calls=%async_computation.3 | async-start | bytes 9437184 | tf_op jit(solution)/shard_map/reduce_scatter | solution.py:13
  292.1 10.6 %copy-start.12 = (bf16[8192,8]{0,1:T(8,128)(2,1)S(1)}, bf16[8192,8]{0,1:T(8,128)(2,1)}, u32[]{:S(2)}) copy-start(bf16[8192,8]{0,1:T(8,128)(2,1)} %param.25) | copy-start | bytes 393220
  299.1 3.6 copy-start.1
  299.1 4.8 copy-start.9
  299.1 4.8 copy-start.13
  303.9 2.0 copy-start.10
  303.9 2.0 copy-start.14
  305.9 1.4 copy-start.8
  305.9 1.8 copy-start.15
  305.9 2.2 copy-start.6
  305.9 2.4 copy-start.2
  306.0 2.4 copy-start.4
  308.4 1.3 copy-start.7
  315.6 173.6 %all-reduce.7.cloned.1.call-start = ((), (), s32[]{:S(2)}) async-start(), calls=%async_computation.6 | async-start | bytes 2097152
Sparse Core Ops, SparseCore 0:
  13.2 112.3 reduce-scatter.2
  128.0 79.3 all-reduce.4
  210.4 81.5 all-gather.2
  315.7 91.7 reduce-scatter.4
  409.7 79.4 all-reduce.6
where the time goes:
time: 498 us
  waiting for transfers between devices  448 us (90%)
  matrix products  21.1 us (4%)
  between operations  14 us (3%)
  local copies, waits for them, and re-layouts  9.28 us (2%)
    reduce_scatter x2, waiting for transfers between devices, own_rows_2(): running = lax.psum_scatter(running, axis, scatter_dimension=0, tiled=True)  204 us
    unnamed x7, waiting for transfers between devices  162 us
    all_gather x1, waiting for transfers between devices, local(): normed_rows = lax.all_gather(normed, TENSOR, axis=0, tiled=True)  81.7 us
  transfers between devices with their start and end apart: 5, of which 5 were waited for; matrix products, arithmetic and copies ran while one was open for 0% of the time, Pallas kernels for 0%

commit v1 on v0

v1 whole, which is shorter than its diff:
```python
import functools
import math

import jax
import jax.numpy as jnp
from jax import lax
from jax.experimental import pallas as pl
from jax.experimental.pallas import tpu as pltpu
from jax.sharding import Mesh
from jax.sharding import PartitionSpec as P

TENSOR = ("tensor_0", "tensor_1")
GROUPS_SEQ_TENSOR = ("groups", "seq", "tensor_0", "tensor_1")
MESH = pl.DeviceIdType.MESH
F32 = jnp.float32
BF16 = jnp.bfloat16
NT = (((1,), (1,)), ((), ()))


def dot(a, b):
    return jnp.dot(a, b, preferred_element_type=F32)


def dot_nt(a, b):
    return lax.dot_general(a, b, NT, preferred_element_type=F32)


def kernel(
    n,
    heads_ref,
    stream_ref,
    projw_ref,
    pscale_ref,
    gain_ref,
    gatew_ref,
    gscale_ref,
    gidx_ref,
    gext_ref,
    upw_ref,
    uscale_ref,
    uidx_ref,
    uext_ref,
    downw_ref,
    dscale_ref,
    didx_ref,
    dext_ref,
    out_ref,
    wcat,
    wd,
    onehot,
    perm,
    gpick,
    upick,
    dextp,
    invg,
    heads_all,
    w_all,
    strm,
    t_sum,
    t_half,
    r_one,
    mixed,
    y_all,
    acc,
    sumsq,
    hid,
    extra_parts,
    ring_s,
    ring_r,
    r_two,
    out_s,
    load_sem,
    heads_ss,
    heads_rs,
    w_ss,
    w_rs,
    strm_ss,
    strm_rs,
    one_ss,
    one_rs,
    aga_ss,
    aga_rs,
    agb_ss,
    agb_rs,
    ring_ss,
    ring_rs,
    two_ss,
    two_rs,
    out_ss,
    out_rs,
):
    feats, tokens = heads_ref.shape
    width = projw_ref.shape[1]
    hidden = gatew_ref.shape[0]
    rows = stream_ref.shape[0]
    slots = gpick.shape[0]
    k_out = gext_ref.shape[0]
    half = width // 2
    strip = half // n
    block = tokens // n
    sub = tokens // 2
    reach = n // 2
    axes = (("tensor_0", "tensor_1"), ("tensor_1", "tensor_0"))
    pos = {name: lax.axis_index(name) for name in TENSOR}
    offsets = sorted(range(1, n), key=lambda r: -min(r, n - r))

    def at(name, shift):
        return lax.rem(pos[name] + (shift + n) % n, n)

    def cols(h, j):
        return pl.ds(pl.multiple_of(h * half + j * strip, strip), strip)

    def send(src, dst, ssem, rsem, name, target):
        return pltpu.make_async_remote_copy(
            src_ref=src,
            dst_ref=dst,
            send_sem=ssem,
            recv_sem=rsem,
            device_id={name: target},
            device_id_type=MESH,
        )

    barrier = pltpu.get_barrier_semaphore()
    for name in TENSOR:
        for r in range(1, n):
            pl.semaphore_signal(
                barrier, inc=1, device_id={name: at(name, r)}, device_id_type=MESH
            )
    loads = [
        pltpu.make_async_copy(gatew_ref, wcat.at[pl.ds(0, hidden), :], load_sem.at[0]),
        pltpu.make_async_copy(upw_ref, wcat.at[pl.ds(slots, hidden), :], load_sem.at[1]),
        pltpu.make_async_copy(downw_ref, wd.at[pl.ds(0, hidden), :], load_sem.at[2]),
    ]
    own_w = []
    for h in (0, 1):
        me = pos[axes[h][0]]
        own_w.append(
            pltpu.make_async_copy(
                projw_ref.at[:, cols(h, me)],
                w_all.at[h, pl.ds(pl.multiple_of(me * feats, feats), feats), :],
                load_sem.at[3 + h],
            )
        )
        own_w[h].start()
    pl.semaphore_wait(barrier, 2 * (n - 1))

    def heads_copy(h, r, sender):
        a = axes[h][0]
        place = pl.ds(pl.multiple_of(sender * feats, feats), feats)
        return send(
            heads_ref,
            heads_all.at[h, place, :],
            heads_ss.at[h, r],
            heads_rs.at[h, r],
            a,
            at(a, r),
        )

    def w_copy(h, r, sender):
        a = axes[h][0]
        place = pl.ds(pl.multiple_of(sender * feats, feats), feats)
        return send(
            projw_ref.at[:, cols(h, at(a, r))],
            w_all.at[h, place, :],
            w_ss.at[h, r],
            w_rs.at[h, r],
            a,
            at(a, r),
        )

    def strm_copy(h, r, sender):
        a = axes[h][0]
        return send(
            stream_ref.at[:, cols(h, at(a, r))],
            strm.at[h, sender],
            strm_ss.at[h, r],
            strm_rs.at[h, r],
            a,
            at(a, r),
        )

    for r in offsets:
        for h in (0, 1):
            heads_copy(h, r, pos[axes[h][0]]).start()
            w_copy(h, r, pos[axes[h][0]]).start()
    for r in offsets:
        for h in (0, 1):
            strm_copy(h, r, pos[axes[h][0]]).start()
    for load in loads:
        load.start()

    for h in (0, 1):
        me = pos[axes[h][0]]
        heads_all[h, pl.ds(pl.multiple_of(me * feats, feats), feats), :] = heads_ref[...]
        strm[h, me] = stream_ref[:, cols(h, me)]
    r_i = lax.broadcasted_iota(jnp.int32, (tokens, tokens), 0)
    c_i = lax.broadcasted_iota(jnp.int32, (tokens, tokens), 1)
    swapped = (
        lax.rem(lax.div(r_i, rows), n) * block + lax.div(r_i, block) * rows + lax.rem(r_i, rows)
    )
    perm[...] = jnp.where(c_i == swapped, 1.0, 0.0).astype(BF16)

    def index_column(idx_ref, count):
        row = lax.rem(lax.broadcasted_iota(jnp.int32, (count, 1), 0), k_out)
        column = jnp.zeros((count, 1), jnp.int32)
        for k in range(k_out):
            column = jnp.where(row == k, idx_ref[0, k], column)
        return column

    for pick, idx_ref in ((gpick, gidx_ref), (upick, uidx_ref)):
        pick[...] = jnp.zeros_like(pick)
        chosen = lax.broadcasted_iota(jnp.int32, (k_out, slots), 1) == index_column(idx_ref, k_out)
        pick[pl.ds(hidden, k_out), :] = jnp.where(chosen, 1.0, 0.0)

    one_rows = onehot.shape[0]
    didx = index_column(didx_ref, one_rows)
    live = lax.broadcasted_iota(jnp.int32, (one_rows, strip), 0) < 2 * k_out

    def prepare(j, carry):
        here = pl.ds(pl.multiple_of(j * strip, strip), strip)
        column = lax.broadcasted_iota(jnp.int32, (one_rows, strip), 1) + j * strip
        onehot[:, here] = jnp.where((column == didx) & live, 1.0, 0.0).astype(BF16)
        blank = jnp.zeros((slots - hidden - k_out, strip), F32)
        for base, ext in ((0, gext_ref), (slots, uext_ref)):
            filled = jnp.concatenate([ext[:, here].astype(F32), blank], axis=0)
            wcat[pl.ds(base + hidden, slots - hidden), here] = filled.astype(BF16)
        wd[pl.ds(hidden, slots - hidden), here] = jnp.zeros((slots - hidden, strip), BF16)
        invg[:, here] = 1.0 / gain_ref[:, here]
        return carry

    lax.fori_loop(0, width // strip, prepare, 0)
    dext = jnp.concatenate([dext_ref[...].astype(F32)] * 2, axis=0)
    dext = jnp.concatenate([dext, jnp.zeros((dextp.shape[0] - 2 * k_out, hidden), F32)], axis=0)
    dextp[...] = jnp.zeros_like(dextp)
    dextp[:, pl.ds(0, hidden)] = dext.astype(BF16)
    acc[...] = jnp.zeros_like(acc)
    sumsq[...] = jnp.zeros_like(sumsq)
    for h in (0, 1):
        for d in (0, 1):
            for m in (0, 1):
                ring_r[h, d, m] = jnp.zeros((sub, strip), BF16)

    def one_copy(h, r):
        b = axes[h][1]
        away = pl.ds(pl.multiple_of(at(b, r) * block, block), block)
        return send(
            t_half.at[h, away, :], r_one.at[h, r], one_ss.at[h, r], one_rs.at[h, r], b, at(b, r)
        )

    for h in (0, 1):
        a = axes[h][0]
        own_w[h].wait()
        for r in offsets:
            heads_copy(h, r, at(a, -r)).wait_recv()
            w_copy(h, r, at(a, -r)).wait_recv()
        if h == 0:
            turn = perm[...]
        else:
            turn = jnp.where(r_i == c_i, 1.0, 0.0).astype(BF16)
        ordered = dot_nt(turn, heads_all[h]).astype(BF16)
        t_sum[h] = dot(ordered, w_all[h])
        t_half[h] = t_sum[h].astype(BF16)
        for r in offsets:
            one_copy(h, r).start()

    def aga_copy(h, r, owner):
        a, b = axes[h]
        place = pl.ds(pl.multiple_of(owner * block, block), block)
        there = y_all.at[h, pos[a], place, :]
        return send(there, there, aga_ss.at[h, r], aga_rs.at[h, r], b, at(b, r))

    for h in (0, 1):
        a, b = axes[h]
        here = cols(h, pos[a])
        own = pl.ds(pl.multiple_of(pos[b] * block, block), block)
        total = t_sum[h, own, :]
        for r in range(1, n):
            one_copy(h, r).wait_recv()
            total += r_one[h, r].astype(F32)
        mixed[h] = total * pscale_ref[:, here]
        for r in range(1, n):
            strm_copy(h, r, at(a, -r)).wait_recv()
        for j in range(n):
            part = pl.ds(j * rows, rows)
            mixed[h, part, :] = mixed[h, part, :] + strm[h, j].astype(F32)
        y_all[h, pos[a], own, :] = (mixed[h] * gain_ref[:, here]).astype(BF16)
        for r in offsets:
            aga_copy(h, r, pos[b]).start()

    def agb_copy(h, d, k, s, strip_id):
        a = axes[h][0]
        there = y_all.at[h, strip_id, pl.ds(s * sub, sub), :]
        return send(
            there, there, agb_ss.at[h, d, k, s], agb_rs.at[h, d, k, s], a, at(a, 1 - 2 * d)
        )

    def behind(h, d, k):
        shift = k if d else n - k
        return lax.rem(pos[axes[h][0]] + shift, n)

    def use(h, j):
        y = y_all[h, j]
        if h == 0:
            y = dot(perm[...], y).astype(BF16)
        here = cols(h, j)
        scaled = y.astype(F32) * invg[:, here]
        scaled = scaled * scaled
        lanes = sumsq.shape[1]
        part = scaled[:, :lanes]
        for q in range(1, strip // lanes):
            part += scaled[:, q * lanes : (q + 1) * lanes]
        sumsq[...] += part
        acc[...] += dot_nt(y, wcat[:, here])

    for h in (0, 1):
        a, b = axes[h]
        for r in range(1, n):
            aga_copy(h, r, at(b, -r)).wait_recv()
        for step in (0, 1):
            for d in (0, 1):
                s = step if d == 0 else 1 - step
                agb_copy(h, d, 0, s, pos[a]).start()
    loads[0].wait()
    loads[1].wait()
    for h in (0, 1):
        use(h, pos[axes[h][0]])

    def gather_step(k, carry):
        for step in (0, 1):
            for h in (0, 1):
                for d in (0, 1):
                    s = step if d == 0 else 1 - step
                    j = behind(h, d, k)
                    agb_copy(h, d, k - 1, s, j).wait_recv()
                    if step == 0:
                        agb_copy(h, d, k, s, j).start()
                    else:

                        @pl.when(k < reach - 1)
                        def _():
                            agb_copy(h, d, k, s, j).start()

        for h in (0, 1):
            for d in (0, 1):
                use(h, behind(h, d, k))
        return carry

    lax.fori_loop(1, reach, gather_step, 0)
    for h in (0, 1):
        j = behind(h, 0, reach)
        agb_copy(h, 0, reach - 1, 0, j).wait_recv()
        agb_copy(h, 1, reach - 1, 1, j).wait_recv()
        use(h, j)

    mean_sq = jnp.sum(sumsq[...], axis=1, keepdims=True) * (1.0 / width)
    factor = lax.rsqrt(mean_sq + 1e-05)

    def branch(base, scale_ref, pick):
        part = acc[:, pl.ds(base, slots)]
        scale = jnp.concatenate([scale_ref[...], jnp.zeros((1, slots - hidden), F32)], axis=1)
        added = jnp.dot(
            part, pick[...], precision=lax.Precision.HIGHEST, preferred_element_type=F32
        )
        return (part * scale + added) * factor

    gate = branch(0, gscale_ref, gpick)
    up = branch(slots, uscale_ref, upick)
    hid[1] = (gate / (1.0 + jnp.exp(-gate)) * up).astype(BF16)
    hid[0] = dot(perm[...], hid[1]).astype(BF16)
    for h in (0, 1):
        added = dot_nt(hid[h], dextp[...])
        high = added.astype(BF16)
        low = (added - high.astype(F32)).astype(BF16)
        lane = lax.broadcasted_iota(jnp.int32, added.shape, 1)
        extra_parts[h] = jnp.where(lane < k_out, high.astype(F32), low.astype(F32)).astype(BF16)
    loads[2].wait()

    def down(h, j, s):
        here = cols(h, j)
        some = pl.ds(pl.multiple_of(s * sub, sub), sub)
        base = dot(hid[h, some, :], wd[:, here]) * dscale_ref[:, here]
        return base + dot(extra_parts[h, some, :], onehot[:, here])

    def ring_copy(h, d, m):
        a = axes[h][0]
        return send(
            ring_s.at[h, d, m],
            ring_r.at[h, d, m + 2],
            ring_ss.at[h, d, m],
            ring_rs.at[h, d, m],
            a,
            at(a, 1 - 2 * d),
        )

    def ring_step(m, carry):
        away = lax.div(n - m, 2)
        for h in (0, 1):
            for d in (0, 1):
                odd = lax.rem(m, 2)
                s = odd if d == 0 else 1 - odd
                shift = n - away if d else away
                j = lax.rem(pos[axes[h][0]] + shift, n)
                value = down(h, j, s)

                @pl.when(m >= 2)
                def _():
                    ring_copy(h, d, m - 2).wait_recv()

                ring_s[h, d, m] = (value + ring_r[h, d, m].astype(F32)).astype(BF16)
                ring_copy(h, d, m).start()
        return carry

    lax.fori_loop(0, n - 1, ring_step, 0)

    def two_copy(h, r):
        b = axes[h][1]
        away = pl.ds(pl.multiple_of(at(b, r) * block, block), block)
        return send(
            t_half.at[h, away, :], r_two.at[h, r], two_ss.at[h, r], two_rs.at[h, r], b, at(b, r)
        )

    for h in (0, 1):
        for r in range(1, n):
            one_copy(h, r).wait_send()
        for s in (0, 1):
            t_sum[h, pl.ds(s * sub, sub), :] = down(h, pos[axes[h][0]], s)
    for h in (0, 1):
        for d in (0, 1):
            for m in (n - 3, n - 2):
                ring_copy(h, d, m).wait_recv()
        for s in (0, 1):
            some = pl.ds(s * sub, sub)
            plus = ring_r[h, 0, n - s].astype(F32)
            minus = ring_r[h, 1, n - 1 + s].astype(F32)
            total = t_sum[h, some, :] + plus + minus
            t_sum[h, some, :] = total
            t_half[h, some, :] = total.astype(BF16)
        for r in offsets:
            two_copy(h, r).start()

    def out_copy(h, r, sender):
        a = axes[h][0]
        return send(
            out_s.at[h, at(a, r)],
            out_ref.at[:, cols(h, sender)],
            out_ss.at[h, r],
            out_rs.at[h, r],
            a,
            at(a, r),
        )

    for h in (0, 1):
        a, b = axes[h]
        own = pl.ds(pl.multiple_of(pos[b] * block, block), block)
        total = t_sum[h, own, :] + mixed[h]
        for r in range(1, n):
            two_copy(h, r).wait_recv()
            total += r_two[h, r].astype(F32)
        mixed[h] = total
        for j in range(n):
            out_s[h, j] = mixed[h, pl.ds(j * rows, rows), :].astype(BF16)
        for r in offsets:
            out_copy(h, r, pos[a]).start()
        out_ref[:, cols(h, pos[a])] = out_s[h, pos[a]]

    for h in (0, 1):
        a, b = axes[h]
        for r in range(1, n):
            heads_copy(h, r, pos[a]).wait_send()
            w_copy(h, r, pos[a]).wait_send()
            strm_copy(h, r, pos[a]).wait_send()
            aga_copy(h, r, pos[b]).wait_send()
            two_copy(h, r).wait_send()
        for d in (0, 1):
            for k in range(reach):
                for s in (0, 1):
                    if k < reach - 1 or s == d:
                        agb_copy(h, d, k, s, behind(h, d, k)).wait_send()
            for m in range(n - 1):
                ring_copy(h, d, m).wait_send()
    for h in (0, 1):
        a = axes[h][0]
        for r in range(1, n):
            out_copy(h, r, pos[a]).wait_send()
            out_copy(h, r, at(a, -r)).wait_recv()


def local(n, *args):
    (
        heads_out,
        stream_in,
        proj_levels,
        proj_scale,
        norm_gain,
        gate_levels,
        gate_scale,
        gate_index,
        gate_extra,
        up_levels,
        up_scale,
        up_index,
        up_extra,
        down_levels,
        down_scale,
        down_index,
        down_extra,
    ) = args
    tokens, feats = heads_out.shape
    rows, width = stream_in.shape
    hidden = gate_levels.shape[1]
    k_out = gate_extra.shape[1]
    slots = -(-(hidden + k_out) // 128) * 128
    strip = width // 2 // n
    block = tokens // n
    sub = tokens // 2
    reach = n // 2
    vmem = pl.BlockSpec(memory_space=pltpu.VMEM)
    smem = pl.BlockSpec(memory_space=pltpu.SMEM)
    hbm = pl.BlockSpec(memory_space=pl.ANY)
    dma = pltpu.SemaphoreType.DMA
    scratch = [
        pltpu.VMEM((2 * slots, width), BF16),
        pltpu.VMEM((slots, width), BF16),
        pltpu.VMEM((128, width), BF16),
        pltpu.VMEM((tokens, tokens), BF16),
        pltpu.VMEM((slots, slots), F32),
        pltpu.VMEM((slots, slots), F32),
        pltpu.VMEM((128, slots), BF16),
        pltpu.VMEM((1, width), F32),
        pltpu.VMEM((2, n * feats, tokens), BF16),
        pltpu.VMEM((2, n * feats, strip), BF16),
        pltpu.VMEM((2, n, rows, strip), BF16),
        pltpu.VMEM((2, tokens, strip), F32),
        pltpu.VMEM((2, tokens, strip), BF16),
        pltpu.VMEM((2, n, block, strip), BF16),
        pltpu.VMEM((2, block, strip), F32),
        pltpu.VMEM((2, n, tokens, strip), BF16),
        pltpu.VMEM((tokens, 2 * slots), F32),
        pltpu.VMEM((tokens, 128), F32),
        pltpu.VMEM((2, tokens, slots), BF16),
        pltpu.VMEM((2, tokens, 128), BF16),
        pltpu.VMEM((2, 2, n - 1, sub, strip), BF16),
        pltpu.VMEM((2, 2, n + 1, sub, strip), BF16),
        pltpu.VMEM((2, n, block, strip), BF16),
        pltpu.VMEM((2, n, rows, strip), BF16),
        dma((5,)),
    ]
    for _ in range(5):
        scratch += [dma((2, n)), dma((2, n))]
    scratch += [dma((2, 2, reach, 2)), dma((2, 2, reach, 2))]
    scratch += [dma((2, 2, n - 1)), dma((2, 2, n - 1))]
    scratch += [dma((2, n)), dma((2, n)), dma((2, n)), dma((2, n))]
    return pl.pallas_call(
        functools.partial(kernel, n),
        out_shape=jax.ShapeDtypeStruct((rows, width), BF16),
        in_specs=[
            vmem, vmem, hbm, vmem, vmem, hbm, vmem, smem, vmem, hbm, vmem, smem, vmem, hbm, vmem, smem, vmem,
        ],
        out_specs=vmem,
        scratch_shapes=scratch,
        compiler_params=pltpu.CompilerParams(
            collective_id=0, has_side_effects=True, vmem_limit_bytes=60 * 1024 * 1024
        ),
    )(
        heads_out.T,
        stream_in,
        proj_levels,
        proj_scale[None, :],
        norm_gain[None, :],
        gate_levels.T,
        gate_scale[None, :],
        gate_index,
        gate_extra.T,
        up_levels.T,
        up_scale[None, :],
        up_index,
        up_extra.T,
        down_levels,
        down_scale[None, :],
        down_index,
        down_extra.T,
    )


def solution(mesh):
    n = math.isqrt(mesh.shape["tensor"])
    torus = Mesh(
        mesh.devices.reshape(mesh.shape["groups"], n, n, mesh.shape["seq"]),
        ("groups", "tensor_0", "tensor_1", "seq"),
    )
    return jax.shard_map(
        functools.partial(local, n),
        mesh=torus,
        in_specs=(
            P(("groups", "seq"), TENSOR),
            P(GROUPS_SEQ_TENSOR, None),
            P(TENSOR, None),
            P(),
            P(),
            P(None, TENSOR),
            P(TENSOR),
            P(TENSOR, None),
            P(None, TENSOR),
            P(None, TENSOR),
            P(TENSOR),
            P(TENSOR, None),
            P(None, TENSOR),
            P(TENSOR, None),
            P(),
            P(TENSOR, None),
            P(TENSOR, None),
        ),
        out_specs=P(GROUPS_SEQ_TENSOR, None),
        check_vma=False,
    )
```

time: 498 us -> 117 us (0.23)
  waiting for transfers between devices: 448 us -> 0 us
  Pallas kernels: 0 us -> 114 us
  matrix products: 21.1 us -> 0 us
  between operations: 14 us -> 0.01 us
  local copies, waits for them, and re-layouts: 9.28 us -> 1.49 us
    reduce_scatter x2 -> x0, waiting for transfers between devices: 204 us -> none  [own_rows_2(): running = lax.psum_scatter(running, axis, scatter_dimension=0, tiled=True)]
    unnamed x7 -> x0, waiting for transfers between devices: 162 us -> none
    pallas_call x0 -> x1, Pallas kernels: none -> 114 us  [local(): pl.pallas_call(functools.partial(kernel, n), out_shape=jax.ShapeDtypeStru...]
    all_gather x1 -> x0, waiting for transfers between devices: 81.7 us -> none  [local(): normed_rows = lax.all_gather(normed, TENSOR, axis=0, tiled=True)]
    dot_general x10 -> x0, matrix products: 21.1 us -> none  [the longest x3 6.59 us: project(): jnp.dot(added, chosen, precision=lax.Precision.HIGHEST)]
    unnamed x36 -> x1, local copies, waits for them, and re-layouts: 9.28 us -> 1.49 us
  transfers between devices with their start and end apart: 5 -> 0, of which waited for: 5 -> 0; matrix products, arithmetic and copies ran while one was open for 0% -> 0% of each run, Pallas kernels for 0% -> 0%
where the time goes in v1:
time: 117 us; the launch traced here: 116 us
  Pallas kernels  114 us (97%)
  local copies, waits for them, and re-layouts  1.49 us (1%)
    pallas_call x1, Pallas kernels, local(): pl.pallas_call(functools.partial(kernel, n), out_shape=jax.ShapeDtypeStru...  114 us

profile of v1, /device:TPU:514, one launch (start us, length us, event | category | flops | bytes accessed | tf_op | source)
XLA Modules:
  0.0 115.7 jit_solution(145076592120772656)
XLA Ops:
  0.0 114.2 %shard_map.163 = bf16[4,8192]{1,0:T(4,128)(2,1)} custom-call(bf16[64,256]{1,0:T(8,128)(2,1)} %bitcast.15, bf16[4,8192]{1,0:T(4,128)(2,1)} %stream_ref.1, bf16[64,8192]{1,0:T(8,128)(2,1)} %projw_ref.1, f32[1,8192]{1,0:T(1,128)} %bitcast.16, f32[1,8192]{1,0:T(1,128)} %bitcast.17, bf16[224,8192]{1,0:T(8,128)(2,1)} %bitcast.11, f32[1,224]{1,0:T(1,128)} %bitcast.20, ...), custom_call_target="tpu_custom_call" | custom-call | tf_op jit(solution)/shard_map/pallas_call | solution.py:553
  114.2 1.5 %copy.19 = bf16[4,8192]{1,0:T(4,128)(2,1)} copy(bf16[4,8192]{1,0:T(4,128)(2,1)} %shard_map.163) | data formatting | bytes 131072

commit v2 on v1

--- a/solution.py
+++ b/solution.py
@@ -27,24 +27,36 @@
 
 def kernel(
     n,
+    cores,
     heads_ref,
     stream_ref,
     projw_ref,
+    pscale_in,
+    gain_in,
+    gatew_ref,
+    gscale_in,
+    gidx_in,
+    gext_in,
+    upw_ref,
+    uscale_in,
+    uidx_in,
+    uext_in,
+    downw_ref,
+    dscale_in,
+    didx_in,
+    dext_in,
+    out_ref,
     pscale_ref,
     gain_ref,
-    gatew_ref,
     gscale_ref,
     gidx_ref,
     gext_ref,
-    upw_ref,
     uscale_ref,
     uidx_ref,
     uext_ref,
-    downw_ref,
     dscale_ref,
     didx_ref,
     dext_ref,
-    out_ref,
     wcat,
     wd,
     onehot,
@@ -74,6 +86,8 @@
     heads_rs,
     w_ss,
     w_rs,
+    share_ss,
+    share_rs,
     strm_ss,
     strm_rs,
     one_ss,
@@ -92,6 +106,7 @@
     feats, tokens = heads_ref.shape
     width = projw_ref.shape[1]
     hidden = gatew_ref.shape[0]
+    part = w_all.shape[2] // cores
     rows = stream_ref.shape[0]
     slots = gpick.shape[0]
     k_out = gext_ref.shape[0]
@@ -120,79 +135,112 @@
             device_id_type=MESH,
         )
 
+    def all_but_one(ref, ssem, rsem, name):
+        return send(ref, ref, ssem, rsem, name, at(name, 1))
+
+    core = lax.axis_index("seq")
     barrier = pltpu.get_barrier_semaphore()
     for name in TENSOR:
         for r in range(1, n):
             pl.semaphore_signal(
                 barrier, inc=1, device_id={name: at(name, r)}, device_id_type=MESH
             )
-    loads = [
-        pltpu.make_async_copy(gatew_ref, wcat.at[pl.ds(0, hidden), :], load_sem.at[0]),
-        pltpu.make_async_copy(upw_ref, wcat.at[pl.ds(slots, hidden), :], load_sem.at[1]),
-        pltpu.make_async_copy(downw_ref, wd.at[pl.ds(0, hidden), :], load_sem.at[2]),
-    ]
-    own_w = []
+    for q in range(1, cores):
+        pl.semaphore_signal(
+            barrier, inc=1, device_id={"seq": lax.rem(core + q, cores)}, device_id_type=MESH
+        )
+
+    def place(sender):
+        return pl.ds(pl.multiple_of(sender * feats, feats), feats)
+
+    mine = pl.ds(pl.multiple_of(core * part, part), part)
+
+    def own_part(h, j):
+        return pl.ds(pl.multiple_of(h * half + j * strip + core * part, part), part)
+
+    first = []
     for h in (0, 1):
         me = pos[axes[h][0]]
-        own_w.append(
-            pltpu.make_async_copy(
-                projw_ref.at[:, cols(h, me)],
-                w_all.at[h, pl.ds(pl.multiple_of(me * feats, feats), feats), :],
-                load_sem.at[3 + h],
-            )
-        )
-        own_w[h].start()
-    pl.semaphore_wait(barrier, 2 * (n - 1))
-
-    def heads_copy(h, r, sender):
-        a = axes[h][0]
-        place = pl.ds(pl.multiple_of(sender * feats, feats), feats)
-        return send(
-            heads_ref,
-            heads_all.at[h, place, :],
-            heads_ss.at[h, r],
-            heads_rs.at[h, r],
+        for src, dst in (
+            (heads_ref, heads_all.at[h, place(me), :]),
+            (projw_ref.at[:, own_part(h, me)], w_all.at[h, place(me), mine]),
+            (stream_ref.at[:, cols(h, me)], strm.at[h, me]),
+        ):
+            first.append(pltpu.make_async_copy(src, dst, load_sem.at[len(first)]))
+            first[-1].start()
+    pl.semaphore_wait(barrier, 2 * (n - 1) + cores - 1)
+
+    def heads_copy(h, r):
+        a = axes[h][0]
+        there = heads_all.at[h, place(pos[a]), :]
+        return send(there, there, heads_ss.at[h], heads_rs.at[h], a, at(a, r))
+
+    def w_copy(h, r):
+        a = axes[h][0]
+        return send(
+            projw_ref.at[:, own_part(h, at(a, r))],
+            w_all.at[h, place(pos[a]), mine],
+            w_ss.at[h],
+            w_rs.at[h],
             a,
             at(a, r),
         )
 
-    def w_copy(h, r, sender):
-        a = axes[h][0]
-        place = pl.ds(pl.multiple_of(sender * feats, feats), feats)
-        return send(
-            projw_ref.at[:, cols(h, at(a, r))],
-            w_all.at[h, place, :],
-            w_ss.at[h, r],
-            w_rs.at[h, r],
+    def share_copy(h, q):
+        there = w_all.at[h, :, mine]
+        return send(
+            there, there, share_ss.at[h, q], share_rs.at[h, q], "seq", lax.rem(core + q, cores)
+        )
+
+    def strm_copy(h, r):
+        a = axes[h][0]
+        return send(
+            stream_ref.at[:, cols(h, at(a, r))],
+            strm.at[h, pos[a]],
+            strm_ss.at[h],
+            strm_rs.at[h],
             a,
             at(a, r),
         )
 
-    def strm_copy(h, r, sender):
-        a = axes[h][0]
-        return send(
-            stream_ref.at[:, cols(h, at(a, r))],
-            strm.at[h, sender],
-            strm_ss.at[h, r],
-            strm_rs.at[h, r],
-            a,
-            at(a, r),
-        )
-
     for r in offsets:
         for h in (0, 1):
-            heads_copy(h, r, pos[axes[h][0]]).start()
-            w_copy(h, r, pos[axes[h][0]]).start()
+            w_copy(h, r).start()
+    for h in (0, 1):
+        first[3 * h].wait()
     for r in offsets:
         for h in (0, 1):
-            strm_copy(h, r, pos[axes[h][0]]).start()
+            heads_copy(h, r).start()
+    for r in offsets:
+        for h in (0, 1):
+            strm_copy(h, r).start()
+    small = []
+    for src, dst in (
+        (pscale_in, pscale_ref),
+        (gain_in, gain_ref),
+        (gscale_in, gscale_ref),
+        (gidx_in, gidx_ref),
+        (gext_in, gext_ref),
+        (uscale_in, uscale_ref),
+        (uidx_in, uidx_ref),
+        (uext_in, uext_ref),
+        (dscale_in, dscale_ref),
+        (didx_in, didx_ref),
+        (dext_in, dext_ref),
+    ):
+        small.append(pltpu.make_async_copy(src, dst, load_sem.at[6 + len(small)]))
+        small[-1].start()
+    base = 6 + len(small)
+    loads = [
+        pltpu.make_async_copy(gatew_ref, wcat.at[pl.ds(0, hidden), :], load_sem.at[base]),
+        pltpu.make_async_copy(upw_ref, wcat.at[pl.ds(slots, hidden), :], load_sem.at[base + 1]),
+        pltpu.make_async_copy(downw_ref, wd.at[pl.ds(0, hidden), :], load_sem.at[base + 2]),
+    ]
     for load in loads:
         load.start()
 
-    for h in (0, 1):
-        me = pos[axes[h][0]]
-        heads_all[h, pl.ds(pl.multiple_of(me * feats, feats), feats), :] = heads_ref[...]
-        strm[h, me] = stream_ref[:, cols(h, me)]
+    for copy in small:
+        copy.wait()
     r_i = lax.broadcasted_iota(jnp.int32, (tokens, tokens), 0)
     c_i = lax.broadcasted_iota(jnp.int32, (tokens, tokens), 1)
     swapped = (
@@ -244,15 +292,21 @@
         b = axes[h][1]
         away = pl.ds(pl.multiple_of(at(b, r) * block, block), block)
         return send(
-            t_half.at[h, away, :], r_one.at[h, r], one_ss.at[h, r], one_rs.at[h, r], b, at(b, r)
-        )
-
-    for h in (0, 1):
-        a = axes[h][0]
-        own_w[h].wait()
-        for r in offsets:
-            heads_copy(h, r, at(a, -r)).wait_recv()
-            w_copy(h, r, at(a, -r)).wait_recv()
+            t_half.at[h, away, :], r_one.at[h, r - 1], one_ss.at[h], one_rs.at[h], b, at(b, r)
+        )
+
+    seen_w = pl.ds(0, (n - 1) * feats)
+    seen_b = pl.ds(0, (n - 1) * block)
+    for h in (0, 1):
+        first[3 * h + 1].wait()
+        all_but_one(w_all.at[h, seen_w, mine], w_ss.at[h], w_rs.at[h], axes[h][0]).wait_recv()
+        for q in range(1, cores):
+            share_copy(h, q).start()
+    for h in (0, 1):
+        a = axes[h][0]
+        all_but_one(heads_all.at[h, seen_w, :], heads_ss.at[h], heads_rs.at[h], a).wait_recv()
+        for q in range(1, cores):
+            share_copy(h, q).wait_recv()
         if h == 0:
             turn = perm[...]
         else:
@@ -265,24 +319,23 @@
 
     def aga_copy(h, r, owner):
         a, b = axes[h]
-        place = pl.ds(pl.multiple_of(owner * block, block), block)
-        there = y_all.at[h, pos[a], place, :]
-        return send(there, there, aga_ss.at[h, r], aga_rs.at[h, r], b, at(b, r))
+        there = y_all.at[h, pos[a], pl.ds(pl.multiple_of(owner * block, block), block), :]
+        return send(there, there, aga_ss.at[h], aga_rs.at[h], b, at(b, r))
 
     for h in (0, 1):
         a, b = axes[h]
         here = cols(h, pos[a])
         own = pl.ds(pl.multiple_of(pos[b] * block, block), block)
         total = t_sum[h, own, :]
+        all_but_one(r_one.at[h], one_ss.at[h], one_rs.at[h], b).wait_recv()
         for r in range(1, n):
-            one_copy(h, r).wait_recv()
-            total += r_one[h, r].astype(F32)
+            total += r_one[h, r - 1].astype(F32)
         mixed[h] = total * pscale_ref[:, here]
-        for r in range(1, n):
-            strm_copy(h, r, at(a, -r)).wait_recv()
+        first[3 * h + 2].wait()
+        all_but_one(strm.at[h, pl.ds(0, n - 1)], strm_ss.at[h], strm_rs.at[h], a).wait_recv()
         for j in range(n):
-            part = pl.ds(j * rows, rows)
-            mixed[h, part, :] = mixed[h, part, :] + strm[h, j].astype(F32)
+            few = pl.ds(j * rows, rows)
+            mixed[h, few, :] = mixed[h, few, :] + strm[h, j].astype(F32)
         y_all[h, pos[a], own, :] = (mixed[h] * gain_ref[:, here]).astype(BF16)
         for r in offsets:
             aga_copy(h, r, pos[b]).start()
@@ -314,8 +367,7 @@
 
     for h in (0, 1):
         a, b = axes[h]
-        for r in range(1, n):
-            aga_copy(h, r, at(b, -r)).wait_recv()
+        all_but_one(y_all.at[h, 0, seen_b, :], aga_ss.at[h], aga_rs.at[h], b).wait_recv()
         for step in (0, 1):
             for d in (0, 1):
                 s = step if d == 0 else 1 - step
@@ -416,12 +468,11 @@
         b = axes[h][1]
         away = pl.ds(pl.multiple_of(at(b, r) * block, block), block)
         return send(
-            t_half.at[h, away, :], r_two.at[h, r], two_ss.at[h, r], two_rs.at[h, r], b, at(b, r)
-        )
-
-    for h in (0, 1):
-        for r in range(1, n):
-            one_copy(h, r).wait_send()
+            t_half.at[h, away, :], r_two.at[h, r - 1], two_ss.at[h], two_rs.at[h], b, at(b, r)
+        )
+
+    for h in (0, 1):
+        all_but_one(r_one.at[h], one_ss.at[h], one_rs.at[h], axes[h][1]).wait_send()
         for s in (0, 1):
             t_sum[h, pl.ds(s * sub, sub), :] = down(h, pos[axes[h][0]], s)
     for h in (0, 1):
@@ -438,39 +489,46 @@
         for r in offsets:
             two_copy(h, r).start()
 
-    def out_copy(h, r, sender):
+    def out_copy(h, r):
         a = axes[h][0]
         return send(
             out_s.at[h, at(a, r)],
-            out_ref.at[:, cols(h, sender)],
-            out_ss.at[h, r],
-            out_rs.at[h, r],
+            out_ref.at[:, cols(h, pos[a])],
+            out_ss.at[h],
+            out_rs.at[h],
             a,
             at(a, r),
         )
 
+    last = []
     for h in (0, 1):
         a, b = axes[h]
         own = pl.ds(pl.multiple_of(pos[b] * block, block), block)
         total = t_sum[h, own, :] + mixed[h]
+        all_but_one(r_two.at[h], two_ss.at[h], two_rs.at[h], b).wait_recv()
         for r in range(1, n):
-            two_copy(h, r).wait_recv()
-            total += r_two[h, r].astype(F32)
+            total += r_two[h, r - 1].astype(F32)
         mixed[h] = total
         for j in range(n):
             out_s[h, j] = mixed[h, pl.ds(j * rows, rows), :].astype(BF16)
         for r in offsets:
-            out_copy(h, r, pos[a]).start()
-        out_ref[:, cols(h, pos[a])] = out_s[h, pos[a]]
+            out_copy(h, r).start()
+        last.append(
+            pltpu.make_async_copy(
+                out_s.at[h, pos[a]], out_ref.at[:, cols(h, pos[a])], load_sem.at[3 * h]
+            )
+        )
+        last[h].start()
 
     for h in (0, 1):
         a, b = axes[h]
-        for r in range(1, n):
-            heads_copy(h, r, pos[a]).wait_send()
-            w_copy(h, r, pos[a]).wait_send()
-            strm_copy(h, r, pos[a]).wait_send()
-            aga_copy(h, r, pos[b]).wait_send()
-            two_copy(h, r).wait_send()
+        all_but_one(heads_all.at[h, seen_w, :], heads_ss.at[h], heads_rs.at[h], a).wait_send()
+        all_but_one(w_all.at[h, seen_w, mine], w_ss.at[h], w_rs.at[h], a).wait_send()
+        for q in range(1, cores):
+            share_copy(h, q).wait_send()
+        all_but_one(strm.at[h, pl.ds(0, n - 1)], strm_ss.at[h], strm_rs.at[h], a).wait_send()
+        all_but_one(y_all.at[h, 0, seen_b, :], aga_ss.at[h], aga_rs.at[h], b).wait_send()
+        all_but_one(r_two.at[h], two_ss.at[h], two_rs.at[h], b).wait_send()
         for d in (0, 1):
             for k in range(reach):
                 for s in (0, 1):
@@ -480,12 +538,13 @@
                 ring_copy(h, d, m).wait_send()
     for h in (0, 1):
         a = axes[h][0]
-        for r in range(1, n):
-            out_copy(h, r, pos[a]).wait_send()
-            out_copy(h, r, at(a, -r)).wait_recv()
-
-
-def local(n, *args):
+        pieces = all_but_one(out_s.at[h, pl.ds(0, n - 1)], out_ss.at[h], out_rs.at[h], a)
+        pieces.wait_send()
+        pieces.wait_recv()
+        last[h].wait()
+
+
+def local(n, cores, *args):
     (
         heads_out,
         stream_in,
@@ -514,11 +573,21 @@
     block = tokens // n
     sub = tokens // 2
     reach = n // 2
-    vmem = pl.BlockSpec(memory_space=pltpu.VMEM)
-    smem = pl.BlockSpec(memory_space=pltpu.SMEM)
+    index = pltpu.SMEM(gate_index.shape, jnp.int32)
     hbm = pl.BlockSpec(memory_space=pl.ANY)
     dma = pltpu.SemaphoreType.DMA
     scratch = [
+        pltpu.VMEM((1, width), F32),
+        pltpu.VMEM((1, width), F32),
+        pltpu.VMEM((1, hidden), F32),
+        index,
+        pltpu.VMEM((k_out, width), BF16),
+        pltpu.VMEM((1, hidden), F32),
+        index,
+        pltpu.VMEM((k_out, width), BF16),
+        pltpu.VMEM((1, width), F32),
+        index,
+        pltpu.VMEM((k_out, hidden), BF16),
         pltpu.VMEM((2 * slots, width), BF16),
         pltpu.VMEM((slots, width), BF16),
         pltpu.VMEM((128, width), BF16),
@@ -532,7 +601,7 @@
         pltpu.VMEM((2, n, rows, strip), BF16),
         pltpu.VMEM((2, tokens, strip), F32),
         pltpu.VMEM((2, tokens, strip), BF16),
-        pltpu.VMEM((2, n, block, strip), BF16),
+        pltpu.VMEM((2, n - 1, block, strip), BF16),
         pltpu.VMEM((2, block, strip), F32),
         pltpu.VMEM((2, n, tokens, strip), BF16),
         pltpu.VMEM((tokens, 2 * slots), F32),
@@ -541,22 +610,20 @@
         pltpu.VMEM((2, tokens, 128), BF16),
         pltpu.VMEM((2, 2, n - 1, sub, strip), BF16),
         pltpu.VMEM((2, 2, n + 1, sub, strip), BF16),
-        pltpu.VMEM((2, n, block, strip), BF16),
+        pltpu.VMEM((2, n - 1, block, strip), BF16),
         pltpu.VMEM((2, n, rows, strip), BF16),
-        dma((5,)),
+        dma((20,)),
     ]
-    for _ in range(5):
-        scratch += [dma((2, n)), dma((2, n))]
+    scratch += [dma((2,)), dma((2,)), dma((2,)), dma((2,)), dma((2, cores)), dma((2, cores))]
+    scratch += [dma((2,)) for _ in range(6)]
     scratch += [dma((2, 2, reach, 2)), dma((2, 2, reach, 2))]
     scratch += [dma((2, 2, n - 1)), dma((2, 2, n - 1))]
-    scratch += [dma((2, n)), dma((2, n)), dma((2, n)), dma((2, n))]
+    scratch += [dma((2,)) for _ in range(4)]
     return pl.pallas_call(
-        functools.partial(kernel, n),
+        functools.partial(kernel, n, cores),
         out_shape=jax.ShapeDtypeStruct((rows, width), BF16),
-        in_specs=[
-            vmem, vmem, hbm, vmem, vmem, hbm, vmem, smem, vmem, hbm, vmem, smem, vmem, hbm, vmem, smem, vmem,
-        ],
-        out_specs=vmem,
+        in_specs=[hbm] * len(args),
+        out_specs=hbm,
         scratch_shapes=scratch,
         compiler_params=pltpu.CompilerParams(
             collective_id=0, has_side_effects=True, vmem_limit_bytes=60 * 1024 * 1024
@@ -589,7 +656,7 @@
         ("groups", "tensor_0", "tensor_1", "seq"),
     )
     return jax.shard_map(
-        functools.partial(local, n),
+        functools.partial(local, n, mesh.shape["seq"]),
         mesh=torus,
         in_specs=(
             P(("groups", "seq"), TENSOR),

time: 117 us -> 109 us (0.932); the launches traced: 116 us -> 109 us
  Pallas kernels: 114 us -> 108 us
    pallas_call x1, Pallas kernels: 114 us -> 108 us  [local(): pl.pallas_call(functools.partial(kernel, n, cores), out_shape=jax.ShapeDt...]
where the time goes in v2:
time: 109 us
  Pallas kernels  108 us (99%)
  local copies, waits for them, and re-layouts  1.49 us (1%)
    pallas_call x1, Pallas kernels, local(): pl.pallas_call(functools.partial(kernel, n, cores), out_shape=jax.ShapeDt...  108 us

profile of v2, /device:TPU:514, one launch (start us, length us, event | category | flops | bytes accessed | tf_op | source)
XLA Modules:
  0.0 109.0 jit_solution(7612340627835741979)
XLA Ops:
  0.0 107.5 %shard_map.163 = bf16[4,8192]{1,0:T(4,128)(2,1)} custom-call(bf16[64,256]{1,0:T(8,128)(2,1)} %bitcast.15, bf16[4,8192]{1,0:T(4,128)(2,1)} %stream_ref.1, bf16[64,8192]{1,0:T(8,128)(2,1)} %projw_ref.1, f32[1,8192]{1,0:T(1,128)} %bitcast.16, f32[1,8192]{1,0:T(1,128)} %bitcast.17, bf16[224,8192]{1,0:T(8,128)(2,1)} %bitcast.11, f32[1,224]{1,0:T(1,128)} %bitcast.20, ...), custom_call_target="tpu_custom_call" | custom-call | tf_op jit(solution)/shard_map/pallas_call | solution.py:622
  107.5 1.5 %copy.19 = bf16[4,8192]{1,0:T(4,128)(2,1)} copy(bf16[4,8192]{1,0:T(4,128)(2,1)} %shard_map.163) | data formatting | bytes 131072

commit v3 on v2

--- a/solution.py
+++ b/solution.py
@@ -79,8 +79,12 @@
     extra_parts,
     ring_s,
     ring_r,
+    two_s,
     r_two,
-    out_s,
+    mix_s,
+    mix_r,
+    down_sum,
+    out_v,
     load_sem,
     heads_ss,
     heads_rs,
@@ -100,8 +104,8 @@
     ring_rs,
     two_ss,
     two_rs,
-    out_ss,
-    out_rs,
+    mix_ss,
+    mix_rs,
 ):
     feats, tokens = heads_ref.shape
     width = projw_ref.shape[1]
@@ -114,6 +118,7 @@
     strip = half // n
     block = tokens // n
     sub = tokens // 2
+    wide = half // 2
     reach = n // 2
     axes = (("tensor_0", "tensor_1"), ("tensor_1", "tensor_0"))
     pos = {name: lax.axis_index(name) for name in TENSOR}
@@ -286,7 +291,7 @@
     for h in (0, 1):
         for d in (0, 1):
             for m in (0, 1):
-                ring_r[h, d, m] = jnp.zeros((sub, strip), BF16)
+                ring_r[h, d, m] = jnp.zeros((block, wide), BF16)
 
     def one_copy(h, r):
         b = axes[h][1]
@@ -321,6 +326,11 @@
         a, b = axes[h]
         there = y_all.at[h, pos[a], pl.ds(pl.multiple_of(owner * block, block), block), :]
         return send(there, there, aga_ss.at[h], aga_rs.at[h], b, at(b, r))
+
+    def mix_copy(h, r):
+        a = axes[h][0]
+        there = mix_r.at[h, :, pl.ds(pl.multiple_of(pos[a] * strip, strip), strip)]
+        return send(mix_s.at[h, at(a, r)], there, mix_ss.at[h], mix_rs.at[h], a, at(a, r))
 
     for h in (0, 1):
         a, b = axes[h]
@@ -339,6 +349,13 @@
         y_all[h, pos[a], own, :] = (mixed[h] * gain_ref[:, here]).astype(BF16)
         for r in offsets:
             aga_copy(h, r, pos[b]).start()
+        for j in range(n):
+            mix_s[h, j] = mixed[h, pl.ds(j * rows, rows), :]
+    for h in (0, 1):
+        me = pos[axes[h][0]]
+        for r in offsets:
+            mix_copy(h, r).start()
+        mix_r[h, :, pl.ds(pl.multiple_of(me * strip, strip), strip)] = mix_s[h, me]
 
     def agb_copy(h, d, k, s, strip_id):
         a = axes[h][0]
@@ -417,8 +434,8 @@
 
     gate = branch(0, gscale_ref, gpick)
     up = branch(slots, uscale_ref, upick)
-    hid[1] = (gate / (1.0 + jnp.exp(-gate)) * up).astype(BF16)
-    hid[0] = dot(perm[...], hid[1]).astype(BF16)
+    hid[0] = (gate / (1.0 + jnp.exp(-gate)) * up).astype(BF16)
+    hid[1] = dot(perm[...], hid[0]).astype(BF16)
     for h in (0, 1):
         added = dot_nt(hid[h], dextp[...])
         high = added.astype(BF16)
@@ -428,8 +445,8 @@
     loads[2].wait()
 
     def down(h, j, s):
-        here = cols(h, j)
-        some = pl.ds(pl.multiple_of(s * sub, sub), sub)
+        here = pl.ds(pl.multiple_of(h * half + s * wide, wide), wide)
+        some = pl.ds(pl.multiple_of(j * block, block), block)
         base = dot(hid[h, some, :], wd[:, here]) * dscale_ref[:, here]
         return base + dot(extra_parts[h, some, :], onehot[:, here])
 
@@ -466,57 +483,39 @@
 
     def two_copy(h, r):
         b = axes[h][1]
-        away = pl.ds(pl.multiple_of(at(b, r) * block, block), block)
         return send(
-            t_half.at[h, away, :], r_two.at[h, r - 1], two_ss.at[h], two_rs.at[h], b, at(b, r)
-        )
-
-    for h in (0, 1):
-        all_but_one(r_one.at[h], one_ss.at[h], one_rs.at[h], axes[h][1]).wait_send()
+            two_s.at[h, at(b, r)], r_two.at[h, r - 1], two_ss.at[h], two_rs.at[h], b, at(b, r)
+        )
+
+    for h in (0, 1):
         for s in (0, 1):
-            t_sum[h, pl.ds(s * sub, sub), :] = down(h, pos[axes[h][0]], s)
+            down_sum[h, :, pl.ds(s * wide, wide)] = down(h, pos[axes[h][0]], s)
     for h in (0, 1):
         for d in (0, 1):
             for m in (n - 3, n - 2):
                 ring_copy(h, d, m).wait_recv()
         for s in (0, 1):
-            some = pl.ds(s * sub, sub)
+            some = pl.ds(s * wide, wide)
             plus = ring_r[h, 0, n - s].astype(F32)
             minus = ring_r[h, 1, n - 1 + s].astype(F32)
-            total = t_sum[h, some, :] + plus + minus
-            t_sum[h, some, :] = total
-            t_half[h, some, :] = total.astype(BF16)
+            down_sum[h, :, some] = down_sum[h, :, some] + plus + minus
+        for j in range(n):
+            two_s[h, j] = down_sum[h, pl.ds(j * rows, rows), :].astype(BF16)
         for r in offsets:
             two_copy(h, r).start()
 
-    def out_copy(h, r):
-        a = axes[h][0]
-        return send(
-            out_s.at[h, at(a, r)],
-            out_ref.at[:, cols(h, pos[a])],
-            out_ss.at[h],
-            out_rs.at[h],
-            a,
-            at(a, r),
-        )
-
     last = []
     for h in (0, 1):
         a, b = axes[h]
-        own = pl.ds(pl.multiple_of(pos[b] * block, block), block)
-        total = t_sum[h, own, :] + mixed[h]
+        all_but_one(mix_s.at[h, pl.ds(0, n - 1)], mix_ss.at[h], mix_rs.at[h], a).wait_recv()
+        total = mix_r[h] + two_s[h, pos[b]].astype(F32)
         all_but_one(r_two.at[h], two_ss.at[h], two_rs.at[h], b).wait_recv()
         for r in range(1, n):
             total += r_two[h, r - 1].astype(F32)
-        mixed[h] = total
-        for j in range(n):
-            out_s[h, j] = mixed[h, pl.ds(j * rows, rows), :].astype(BF16)
-        for r in offsets:
-            out_copy(h, r).start()
+        here = pl.ds(h * half, half)
+        out_v[:, here] = total.astype(BF16)
         last.append(
-            pltpu.make_async_copy(
-                out_s.at[h, pos[a]], out_ref.at[:, cols(h, pos[a])], load_sem.at[3 * h]
-            )
+            pltpu.make_async_copy(out_v.at[:, here], out_ref.at[:, here], load_sem.at[3 * h])
         )
         last[h].start()
 
@@ -528,6 +527,8 @@
             share_copy(h, q).wait_send()
         all_but_one(strm.at[h, pl.ds(0, n - 1)], strm_ss.at[h], strm_rs.at[h], a).wait_send()
         all_but_one(y_all.at[h, 0, seen_b, :], aga_ss.at[h], aga_rs.at[h], b).wait_send()
+        all_but_one(r_one.at[h], one_ss.at[h], one_rs.at[h], b).wait_send()
+        all_but_one(mix_s.at[h, pl.ds(0, n - 1)], mix_ss.at[h], mix_rs.at[h], a).wait_send()
         all_but_one(r_two.at[h], two_ss.at[h], two_rs.at[h], b).wait_send()
         for d in (0, 1):
             for k in range(reach):
@@ -536,12 +537,8 @@
                         agb_copy(h, d, k, s, behind(h, d, k)).wait_send()
             for m in range(n - 1):
                 ring_copy(h, d, m).wait_send()
-    for h in (0, 1):
-        a = axes[h][0]
-        pieces = all_but_one(out_s.at[h, pl.ds(0, n - 1)], out_ss.at[h], out_rs.at[h], a)
-        pieces.wait_send()
-        pieces.wait_recv()
-        last[h].wait()
+    for copy in last:
+        copy.wait()
 
 
 def local(n, cores, *args):
@@ -571,7 +568,6 @@
     slots = -(-(hidden + k_out) // 128) * 128
     strip = width // 2 // n
     block = tokens // n
-    sub = tokens // 2
     reach = n // 2
     index = pltpu.SMEM(gate_index.shape, jnp.int32)
     hbm = pl.BlockSpec(memory_space=pl.ANY)
@@ -608,10 +604,14 @@
         pltpu.VMEM((tokens, 128), F32),
         pltpu.VMEM((2, tokens, slots), BF16),
         pltpu.VMEM((2, tokens, 128), BF16),
-        pltpu.VMEM((2, 2, n - 1, sub, strip), BF16),
-        pltpu.VMEM((2, 2, n + 1, sub, strip), BF16),
-        pltpu.VMEM((2, n - 1, block, strip), BF16),
-        pltpu.VMEM((2, n, rows, strip), BF16),
+        pltpu.VMEM((2, 2, n - 1, block, width // 4), BF16),
+        pltpu.VMEM((2, 2, n + 1, block, width // 4), BF16),
+        pltpu.VMEM((2, n, rows, width // 2), BF16),
+        pltpu.VMEM((2, n - 1, rows, width // 2), BF16),
+        pltpu.VMEM((2, n, rows, strip), F32),
+        pltpu.VMEM((2, rows, width // 2), F32),
+        pltpu.VMEM((2, block, width // 2), F32),
+        pltpu.VMEM((rows, width), BF16),
         dma((20,)),
     ]
     scratch += [dma((2,)), dma((2,)), dma((2,)), dma((2,)), dma((2, cores)), dma((2, cores))]

time: 109 us -> 105 us (0.963)
  Pallas kernels: 108 us -> 103 us
    pallas_call x1, Pallas kernels: 108 us -> 103 us  [local(): pl.pallas_call(functools.partial(kernel, n, cores), out_shape=jax.ShapeDt...]
where the time goes in v3:
time: 105 us
  Pallas kernels  103 us (98%)
  local copies, waits for them, and re-layouts  1.49 us (1%)
    pallas_call x1, Pallas kernels, local(): pl.pallas_call(functools.partial(kernel, n, cores), out_shape=jax.ShapeDt...  103 us

profile of v3, /device:TPU:514, one launch (start us, length us, event | category | flops | bytes accessed | tf_op | source)
XLA Modules:
  0.0 105.0 jit_solution(11333600589875532805)
XLA Ops:
  0.0 103.5 %shard_map.163 = bf16[4,8192]{1,0:T(4,128)(2,1)} custom-call(bf16[64,256]{1,0:T(8,128)(2,1)} %bitcast.15, bf16[4,8192]{1,0:T(4,128)(2,1)} %stream_ref.1, bf16[64,8192]{1,0:T(8,128)(2,1)} %projw_ref.1, f32[1,8192]{1,0:T(1,128)} %bitcast.16, f32[1,8192]{1,0:T(1,128)} %bitcast.17, bf16[224,8192]{1,0:T(8,128)(2,1)} %bitcast.11, f32[1,224]{1,0:T(1,128)} %bitcast.20, ...), custom_call_target="tpu_custom_call" | custom-call | tf_op jit(solution)/shard_map/pallas_call | solution.py:622
  103.5 1.5 %copy.19 = bf16[4,8192]{1,0:T(4,128)(2,1)} copy(bf16[4,8192]{1,0:T(4,128)(2,1)} %shard_map.163) | data formatting | bytes 131072

commit v4 on v3

--- a/solution.py
+++ b/solution.py
@@ -66,6 +66,7 @@
     dextp,
     invg,
     heads_all,
+    ordered,
     w_all,
     strm,
     t_sum,
@@ -110,7 +111,9 @@
     feats, tokens = heads_ref.shape
     width = projw_ref.shape[1]
     hidden = gatew_ref.shape[0]
-    part = w_all.shape[2] // cores
+    chunks = w_all.shape[1]
+    chunk = w_all.shape[3]
+    part = chunk // cores
     rows = stream_ref.shape[0]
     slots = gpick.shape[0]
     k_out = gext_ref.shape[0]
@@ -160,16 +163,22 @@
 
     mine = pl.ds(pl.multiple_of(core * part, part), part)
 
-    def own_part(h, j):
-        return pl.ds(pl.multiple_of(h * half + j * strip + core * part, part), part)
+    def some_cols(h, j, c):
+        return pl.ds(pl.multiple_of(h * half + j * strip + c * chunk, chunk), chunk)
+
+    def own_part(h, j, c):
+        start = h * half + j * strip + c * chunk + core * part
+        return pl.ds(pl.multiple_of(start, part), part)
 
     first = []
     for h in (0, 1):
         me = pos[axes[h][0]]
         for src, dst in (
             (heads_ref, heads_all.at[h, place(me), :]),
-            (projw_ref.at[:, own_part(h, me)], w_all.at[h, place(me), mine]),
             (stream_ref.at[:, cols(h, me)], strm.at[h, me]),
+        ) + tuple(
+            (projw_ref.at[:, own_part(h, me, c)], w_all.at[h, c, place(me), mine])
+            for c in range(chunks)
         ):
             first.append(pltpu.make_async_copy(src, dst, load_sem.at[len(first)]))
             first[-1].start()
@@ -180,22 +189,21 @@
         there = heads_all.at[h, place(pos[a]), :]
         return send(there, there, heads_ss.at[h], heads_rs.at[h], a, at(a, r))
 
-    def w_copy(h, r):
+    def w_copy(h, c, r):
         a = axes[h][0]
         return send(
-            projw_ref.at[:, own_part(h, at(a, r))],
-            w_all.at[h, place(pos[a]), mine],
-            w_ss.at[h],
-            w_rs.at[h],
+            projw_ref.at[:, own_part(h, at(a, r), c)],
+            w_all.at[h, c, place(pos[a]), mine],
+            w_ss.at[h, c],
+            w_rs.at[h, c],
             a,
             at(a, r),
         )
 
-    def share_copy(h, q):
-        there = w_all.at[h, :, mine]
-        return send(
-            there, there, share_ss.at[h, q], share_rs.at[h, q], "seq", lax.rem(core + q, cores)
-        )
+    def share_copy(h, c, q):
+        there = w_all.at[h, c, :, mine]
+        to = lax.rem(core + q, cores)
+        return send(there, there, share_ss.at[h, c, q], share_rs.at[h, c, q], "seq", to)
 
     def strm_copy(h, r):
         a = axes[h][0]
@@ -208,14 +216,17 @@
             at(a, r),
         )
 
-    for r in offsets:
-        for h in (0, 1):
-            w_copy(h, r).start()
-    for h in (0, 1):
-        first[3 * h].wait()
-    for r in offsets:
-        for h in (0, 1):
-            heads_copy(h, r).start()
+    each = 2 + chunks
+    for c in range(chunks):
+        for r in offsets:
+            for h in (0, 1):
+                w_copy(h, c, r).start()
+        if c == 0:
+            for h in (0, 1):
+                first[each * h].wait()
+            for r in offsets:
+                for h in (0, 1):
+                    heads_copy(h, r).start()
     for r in offsets:
         for h in (0, 1):
             strm_copy(h, r).start()
@@ -233,9 +244,9 @@
         (didx_in, didx_ref),
         (dext_in, dext_ref),
     ):
-        small.append(pltpu.make_async_copy(src, dst, load_sem.at[6 + len(small)]))
+        small.append(pltpu.make_async_copy(src, dst, load_sem.at[len(first) + len(small)]))
         small[-1].start()
-    base = 6 + len(small)
+    base = len(first) + len(small)
     loads = [
         pltpu.make_async_copy(gatew_ref, wcat.at[pl.ds(0, hidden), :], load_sem.at[base]),
         pltpu.make_async_copy(upw_ref, wcat.at[pl.ds(slots, hidden), :], load_sem.at[base + 1]),
@@ -293,75 +304,94 @@
             for m in (0, 1):
                 ring_r[h, d, m] = jnp.zeros((block, wide), BF16)
 
-    def one_copy(h, r):
+    def one_copy(h, c, r):
         b = axes[h][1]
         away = pl.ds(pl.multiple_of(at(b, r) * block, block), block)
         return send(
-            t_half.at[h, away, :], r_one.at[h, r - 1], one_ss.at[h], one_rs.at[h], b, at(b, r)
+            t_half.at[h, c, away, :],
+            r_one.at[h, c, r - 1],
+            one_ss.at[h, c],
+            one_rs.at[h, c],
+            b,
+            at(b, r),
         )
 
     seen_w = pl.ds(0, (n - 1) * feats)
     seen_b = pl.ds(0, (n - 1) * block)
-    for h in (0, 1):
-        first[3 * h + 1].wait()
-        all_but_one(w_all.at[h, seen_w, mine], w_ss.at[h], w_rs.at[h], axes[h][0]).wait_recv()
-        for q in range(1, cores):
-            share_copy(h, q).start()
-    for h in (0, 1):
-        a = axes[h][0]
-        all_but_one(heads_all.at[h, seen_w, :], heads_ss.at[h], heads_rs.at[h], a).wait_recv()
-        for q in range(1, cores):
-            share_copy(h, q).wait_recv()
-        if h == 0:
-            turn = perm[...]
-        else:
-            turn = jnp.where(r_i == c_i, 1.0, 0.0).astype(BF16)
-        ordered = dot_nt(turn, heads_all[h]).astype(BF16)
-        t_sum[h] = dot(ordered, w_all[h])
-        t_half[h] = t_sum[h].astype(BF16)
-        for r in offsets:
-            one_copy(h, r).start()
-
-    def aga_copy(h, r, owner):
+    for c in range(chunks):
+        for h in (0, 1):
+            a = axes[h][0]
+            first[each * h + 2 + c].wait()
+            all_but_one(
+                w_all.at[h, c, seen_w, mine], w_ss.at[h, c], w_rs.at[h, c], a
+            ).wait_recv()
+            for q in range(1, cores):
+                share_copy(h, c, q).start()
+        for h in (0, 1):
+            a = axes[h][0]
+            if c == 0:
+                all_but_one(
+                    heads_all.at[h, seen_w, :], heads_ss.at[h], heads_rs.at[h], a
+                ).wait_recv()
+                if h == 0:
+                    turn = perm[...]
+                else:
+                    turn = jnp.where(r_i == c_i, 1.0, 0.0).astype(BF16)
+                ordered[h] = dot_nt(turn, heads_all[h]).astype(BF16)
+            for q in range(1, cores):
+                share_copy(h, c, q).wait_recv()
+            t_sum[h, c] = dot(ordered[h], w_all[h, c])
+            t_half[h, c] = t_sum[h, c].astype(BF16)
+            for r in offsets:
+                one_copy(h, c, r).start()
+
+    def aga_copy(h, c, r):
         a, b = axes[h]
-        there = y_all.at[h, pos[a], pl.ds(pl.multiple_of(owner * block, block), block), :]
-        return send(there, there, aga_ss.at[h], aga_rs.at[h], b, at(b, r))
+        own = pl.ds(pl.multiple_of(pos[b] * block, block), block)
+        there = y_all.at[h, pos[a], c, own, :]
+        return send(there, there, aga_ss.at[h, c], aga_rs.at[h, c], b, at(b, r))
 
     def mix_copy(h, r):
         a = axes[h][0]
         there = mix_r.at[h, :, pl.ds(pl.multiple_of(pos[a] * strip, strip), strip)]
         return send(mix_s.at[h, at(a, r)], there, mix_ss.at[h], mix_rs.at[h], a, at(a, r))
 
-    for h in (0, 1):
-        a, b = axes[h]
-        here = cols(h, pos[a])
-        own = pl.ds(pl.multiple_of(pos[b] * block, block), block)
-        total = t_sum[h, own, :]
-        all_but_one(r_one.at[h], one_ss.at[h], one_rs.at[h], b).wait_recv()
-        for r in range(1, n):
-            total += r_one[h, r - 1].astype(F32)
-        mixed[h] = total * pscale_ref[:, here]
-        first[3 * h + 2].wait()
-        all_but_one(strm.at[h, pl.ds(0, n - 1)], strm_ss.at[h], strm_rs.at[h], a).wait_recv()
-        for j in range(n):
-            few = pl.ds(j * rows, rows)
-            mixed[h, few, :] = mixed[h, few, :] + strm[h, j].astype(F32)
-        y_all[h, pos[a], own, :] = (mixed[h] * gain_ref[:, here]).astype(BF16)
-        for r in offsets:
-            aga_copy(h, r, pos[b]).start()
-        for j in range(n):
-            mix_s[h, j] = mixed[h, pl.ds(j * rows, rows), :]
+    for c in range(chunks):
+        for h in (0, 1):
+            a, b = axes[h]
+            here = some_cols(h, pos[a], c)
+            within = pl.ds(c * chunk, chunk)
+            own = pl.ds(pl.multiple_of(pos[b] * block, block), block)
+            total = t_sum[h, c, own, :]
+            if c == 0:
+                first[each * h + 1].wait()
+                all_but_one(
+                    strm.at[h, pl.ds(0, n - 1)], strm_ss.at[h], strm_rs.at[h], a
+                ).wait_recv()
+            all_but_one(r_one.at[h, c], one_ss.at[h, c], one_rs.at[h, c], b).wait_recv()
+            for r in range(1, n):
+                total += r_one[h, c, r - 1].astype(F32)
+            mixed[h, c] = total * pscale_ref[:, here]
+            for j in range(n):
+                few = pl.ds(j * rows, rows)
+                mixed[h, c, few, :] = mixed[h, c, few, :] + strm[h, j, :, within].astype(F32)
+            y_all[h, pos[a], c, own, :] = (mixed[h, c] * gain_ref[:, here]).astype(BF16)
+            for r in offsets:
+                aga_copy(h, c, r).start()
+            for j in range(n):
+                mix_s[h, j, :, within] = mixed[h, c, pl.ds(j * rows, rows), :]
     for h in (0, 1):
         me = pos[axes[h][0]]
         for r in offsets:
             mix_copy(h, r).start()
         mix_r[h, :, pl.ds(pl.multiple_of(me * strip, strip), strip)] = mix_s[h, me]
 
-    def agb_copy(h, d, k, s, strip_id):
+    def agb_copy(h, d, k, c, strip_id, whole):
         a = axes[h][0]
-        there = y_all.at[h, strip_id, pl.ds(s * sub, sub), :]
+        some = pl.ds(0, tokens) if whole else pl.ds(d * sub, sub)
+        there = y_all.at[h, strip_id, c, some, :]
         return send(
-            there, there, agb_ss.at[h, d, k, s], agb_rs.at[h, d, k, s], a, at(a, 1 - 2 * d)
+            there, there, agb_ss.at[h, d, k, c], agb_rs.at[h, d, k, c], a, at(a, 1 - 2 * d)
         )
 
     def behind(h, d, k):
@@ -369,45 +399,49 @@
         return lax.rem(pos[axes[h][0]] + shift, n)
 
     def use(h, j):
-        y = y_all[h, j]
-        if h == 0:
-            y = dot(perm[...], y).astype(BF16)
-        here = cols(h, j)
-        scaled = y.astype(F32) * invg[:, here]
-        scaled = scaled * scaled
         lanes = sumsq.shape[1]
-        part = scaled[:, :lanes]
-        for q in range(1, strip // lanes):
-            part += scaled[:, q * lanes : (q + 1) * lanes]
-        sumsq[...] += part
-        acc[...] += dot_nt(y, wcat[:, here])
-
-    for h in (0, 1):
-        a, b = axes[h]
-        all_but_one(y_all.at[h, 0, seen_b, :], aga_ss.at[h], aga_rs.at[h], b).wait_recv()
-        for step in (0, 1):
+        squares = sumsq[...]
+        total = acc[...]
+        for c in range(chunks):
+            y = y_all[h, j, c]
+            if h == 0:
+                y = dot(perm[...], y).astype(BF16)
+            here = some_cols(h, j, c)
+            scaled = y.astype(F32) * invg[:, here]
+            scaled = scaled * scaled
+            for q in range(chunk // lanes):
+                squares += scaled[:, q * lanes : (q + 1) * lanes]
+            total += dot_nt(y, wcat[:, here])
+        sumsq[...] = squares
+        acc[...] = total
+
+    for c in range(chunks):
+        for h in (0, 1):
+            a, b = axes[h]
+            all_but_one(
+                y_all.at[h, 0, c, seen_b, :], aga_ss.at[h, c], aga_rs.at[h, c], b
+            ).wait_recv()
             for d in (0, 1):
-                s = step if d == 0 else 1 - step
-                agb_copy(h, d, 0, s, pos[a]).start()
+                agb_copy(h, d, 0, c, pos[a], True).start()
     loads[0].wait()
     loads[1].wait()
     for h in (0, 1):
         use(h, pos[axes[h][0]])
 
     def gather_step(k, carry):
-        for step in (0, 1):
+        for c in range(chunks):
             for h in (0, 1):
                 for d in (0, 1):
-                    s = step if d == 0 else 1 - step
                     j = behind(h, d, k)
-                    agb_copy(h, d, k - 1, s, j).wait_recv()
-                    if step == 0:
-                        agb_copy(h, d, k, s, j).start()
-                    else:
-
-                        @pl.when(k < reach - 1)
-                        def _():
-                            agb_copy(h, d, k, s, j).start()
+                    agb_copy(h, d, k - 1, c, j, True).wait_recv()
+
+                    @pl.when(k < reach - 1)
+                    def _():
+                        agb_copy(h, d, k, c, j, True).start()
+
+                    @pl.when(k == reach - 1)
+                    def _():
+                        agb_copy(h, d, k, c, j, False).start()
 
         for h in (0, 1):
             for d in (0, 1):
@@ -417,8 +451,9 @@
     lax.fori_loop(1, reach, gather_step, 0)
     for h in (0, 1):
         j = behind(h, 0, reach)
-        agb_copy(h, 0, reach - 1, 0, j).wait_recv()
-        agb_copy(h, 1, reach - 1, 1, j).wait_recv()
+        for d in (0, 1):
+            for c in range(chunks):
+                agb_copy(h, d, reach - 1, c, j, False).wait_recv()
         use(h, j)
 
     mean_sq = jnp.sum(sumsq[...], axis=1, keepdims=True) * (1.0 / width)
@@ -522,19 +557,23 @@
     for h in (0, 1):
         a, b = axes[h]
         all_but_one(heads_all.at[h, seen_w, :], heads_ss.at[h], heads_rs.at[h], a).wait_send()
-        all_but_one(w_all.at[h, seen_w, mine], w_ss.at[h], w_rs.at[h], a).wait_send()
-        for q in range(1, cores):
-            share_copy(h, q).wait_send()
         all_but_one(strm.at[h, pl.ds(0, n - 1)], strm_ss.at[h], strm_rs.at[h], a).wait_send()
-        all_but_one(y_all.at[h, 0, seen_b, :], aga_ss.at[h], aga_rs.at[h], b).wait_send()
-        all_but_one(r_one.at[h], one_ss.at[h], one_rs.at[h], b).wait_send()
+        for c in range(chunks):
+            all_but_one(
+                w_all.at[h, c, seen_w, mine], w_ss.at[h, c], w_rs.at[h, c], a
+            ).wait_send()
+            for q in range(1, cores):
+                share_copy(h, c, q).wait_send()
+            all_but_one(
+                y_all.at[h, 0, c, seen_b, :], aga_ss.at[h, c], aga_rs.at[h, c], b
+            ).wait_send()
+            all_but_one(r_one.at[h, c], one_ss.at[h, c], one_rs.at[h, c], b).wait_send()
         all_but_one(mix_s.at[h, pl.ds(0, n - 1)], mix_ss.at[h], mix_rs.at[h], a).wait_send()
         all_but_one(r_two.at[h], two_ss.at[h], two_rs.at[h], b).wait_send()
         for d in (0, 1):
             for k in range(reach):
-                for s in (0, 1):
-                    if k < reach - 1 or s == d:
-                        agb_copy(h, d, k, s, behind(h, d, k)).wait_send()
+                for c in range(chunks):
+                    agb_copy(h, d, k, c, behind(h, d, k), k < reach - 1).wait_send()
             for m in range(n - 1):
                 ring_copy(h, d, m).wait_send()
     for copy in last:
@@ -567,6 +606,8 @@
     k_out = gate_extra.shape[1]
     slots = -(-(hidden + k_out) // 128) * 128
     strip = width // 2 // n
+    chunks = 2
+    chunk = strip // chunks
     block = tokens // n
     reach = n // 2
     index = pltpu.SMEM(gate_index.shape, jnp.int32)
@@ -593,13 +634,14 @@
         pltpu.VMEM((128, slots), BF16),
         pltpu.VMEM((1, width), F32),
         pltpu.VMEM((2, n * feats, tokens), BF16),
-        pltpu.VMEM((2, n * feats, strip), BF16),
+        pltpu.VMEM((2, tokens, n * feats), BF16),
+        pltpu.VMEM((2, chunks, n * feats, chunk), BF16),
         pltpu.VMEM((2, n, rows, strip), BF16),
-        pltpu.VMEM((2, tokens, strip), F32),
-        pltpu.VMEM((2, tokens, strip), BF16),
-        pltpu.VMEM((2, n - 1, block, strip), BF16),
-        pltpu.VMEM((2, block, strip), F32),
-        pltpu.VMEM((2, n, tokens, strip), BF16),
+        pltpu.VMEM((2, chunks, tokens, chunk), F32),
+        pltpu.VMEM((2, chunks, tokens, chunk), BF16),
+        pltpu.VMEM((2, chunks, n - 1, block, chunk), BF16),
+        pltpu.VMEM((2, chunks, block, chunk), F32),
+        pltpu.VMEM((2, n, chunks, tokens, chunk), BF16),
         pltpu.VMEM((tokens, 2 * slots), F32),
         pltpu.VMEM((tokens, 128), F32),
         pltpu.VMEM((2, tokens, slots), BF16),
@@ -612,11 +654,12 @@
         pltpu.VMEM((2, rows, width // 2), F32),
         pltpu.VMEM((2, block, width // 2), F32),
         pltpu.VMEM((rows, width), BF16),
-        dma((20,)),
+        dma((4 + 2 * chunks + 14,)),
     ]
-    scratch += [dma((2,)), dma((2,)), dma((2,)), dma((2,)), dma((2, cores)), dma((2, cores))]
-    scratch += [dma((2,)) for _ in range(6)]
-    scratch += [dma((2, 2, reach, 2)), dma((2, 2, reach, 2))]
+    scratch += [dma((2,)), dma((2,)), dma((2, chunks)), dma((2, chunks))]
+    scratch += [dma((2, chunks, cores)), dma((2, chunks, cores)), dma((2,)), dma((2,))]
+    scratch += [dma((2, chunks)) for _ in range(4)]
+    scratch += [dma((2, 2, reach, chunks)), dma((2, 2, reach, chunks))]
     scratch += [dma((2, 2, n - 1)), dma((2, 2, n - 1))]
     scratch += [dma((2,)) for _ in range(4)]
     return pl.pallas_call(

time: 105 us -> 104 us (level)
    pallas_call x1, Pallas kernels: 103 us -> 102 us  [local(): pl.pallas_call(functools.partial(kernel, n, cores), out_shape=jax.ShapeDt...]
where the time goes in v4:
time: 104 us
  Pallas kernels  102 us (98%)
  local copies, waits for them, and re-layouts  1.49 us (1%)
    pallas_call x1, Pallas kernels, local(): pl.pallas_call(functools.partial(kernel, n, cores), out_shape=jax.ShapeDt...  102 us

profile of v4, /device:TPU:514, one launch (start us, length us, event | category | flops | bytes accessed | tf_op | source)
XLA Modules:
  0.0 103.6 jit_solution(4923323728685519957)
XLA Ops:
  0.0 102.1 %shard_map.163 = bf16[4,8192]{1,0:T(4,128)(2,1)} custom-call(bf16[64,256]{1,0:T(8,128)(2,1)} %bitcast.15, bf16[4,8192]{1,0:T(4,128)(2,1)} %stream_ref.1, bf16[64,8192]{1,0:T(8,128)(2,1)} %projw_ref.1, f32[1,8192]{1,0:T(1,128)} %bitcast.16, f32[1,8192]{1,0:T(1,128)} %bitcast.17, bf16[224,8192]{1,0:T(8,128)(2,1)} %bitcast.11, f32[1,224]{1,0:T(1,128)} %bitcast.20, ...), custom_call_target="tpu_custom_call" | custom-call | tf_op jit(solution)/shard_map/pallas_call | solution.py:665
  102.1 1.5 %copy.19 = bf16[4,8192]{1,0:T(4,128)(2,1)} copy(bf16[4,8192]{1,0:T(4,128)(2,1)} %shard_map.163) | data formatting | bytes 131072

commit v5 on v4

--- a/solution.py
+++ b/solution.py
@@ -121,7 +121,10 @@
     strip = half // n
     block = tokens // n
     sub = tokens // 2
-    wide = half // 2
+    wide = ring_s.shape[4]
+    pieces = half // wide
+    per = pieces // 2
+    messages = per * (n - 1)
     reach = n // 2
     axes = (("tensor_0", "tensor_1"), ("tensor_1", "tensor_0"))
     pos = {name: lax.axis_index(name) for name in TENSOR}
@@ -184,10 +187,23 @@
             first[-1].start()
     pl.semaphore_wait(barrier, 2 * (n - 1) + cores - 1)
 
-    def heads_copy(h, r):
+    def behind(h, d, k):
+        shift = k if d else n - k
+        return lax.rem(pos[axes[h][0]] + shift, n)
+
+    def heads_copy(h, d, k):
         a = axes[h][0]
-        there = heads_all.at[h, place(pos[a]), :]
-        return send(there, there, heads_ss.at[h], heads_rs.at[h], a, at(a, r))
+        few = feats // 2 if k == reach - 1 else feats
+        start = behind(h, d, k) * feats + (d * few if k == reach - 1 else 0)
+        there = heads_all.at[h, pl.ds(pl.multiple_of(start, few), few), :]
+        return send(there, there, heads_ss.at[h, d, k], heads_rs.at[h, d, k], a, at(a, 1 - 2 * d))
+
+    def heads_arrive(k):
+        for h in (0, 1):
+            for d in (0, 1):
+                heads_copy(h, d, k).wait_recv()
+                if k < reach - 1:
+                    heads_copy(h, d, k + 1).start()
 
     def w_copy(h, c, r):
         a = axes[h][0]
@@ -217,19 +233,13 @@
         )
 
     each = 2 + chunks
-    for c in range(chunks):
-        for r in offsets:
-            for h in (0, 1):
-                w_copy(h, c, r).start()
-        if c == 0:
-            for h in (0, 1):
-                first[each * h].wait()
-            for r in offsets:
-                for h in (0, 1):
-                    heads_copy(h, r).start()
+    for h in (0, 1):
+        first[each * h].wait()
+        for d in (0, 1):
+            heads_copy(h, d, 0).start()
     for r in offsets:
         for h in (0, 1):
-            strm_copy(h, r).start()
+            w_copy(h, 0, r).start()
     small = []
     for src, dst in (
         (pscale_in, pscale_ref),
@@ -255,6 +265,15 @@
     for load in loads:
         load.start()
 
+    heads_arrive(0)
+    for c in range(1, chunks):
+        for r in offsets:
+            for h in (0, 1):
+                w_copy(h, c, r).start()
+    for r in offsets:
+        for h in (0, 1):
+            strm_copy(h, r).start()
+
     for copy in small:
         copy.wait()
     r_i = lax.broadcasted_iota(jnp.int32, (tokens, tokens), 0)
@@ -301,7 +320,7 @@
     sumsq[...] = jnp.zeros_like(sumsq)
     for h in (0, 1):
         for d in (0, 1):
-            for m in (0, 1):
+            for m in range(pieces):
                 ring_r[h, d, m] = jnp.zeros((block, wide), BF16)
 
     def one_copy(h, c, r):
@@ -318,6 +337,8 @@
 
     seen_w = pl.ds(0, (n - 1) * feats)
     seen_b = pl.ds(0, (n - 1) * block)
+    for k in range(1, reach - 1):
+        heads_arrive(k)
     for c in range(chunks):
         for h in (0, 1):
             a = axes[h][0]
@@ -330,9 +351,8 @@
         for h in (0, 1):
             a = axes[h][0]
             if c == 0:
-                all_but_one(
-                    heads_all.at[h, seen_w, :], heads_ss.at[h], heads_rs.at[h], a
-                ).wait_recv()
+                for d in (0, 1):
+                    heads_copy(h, d, reach - 1).wait_recv()
                 if h == 0:
                     turn = perm[...]
                 else:
@@ -394,10 +414,6 @@
             there, there, agb_ss.at[h, d, k, c], agb_rs.at[h, d, k, c], a, at(a, 1 - 2 * d)
         )
 
-    def behind(h, d, k):
-        shift = k if d else n - k
-        return lax.rem(pos[axes[h][0]] + shift, n)
-
     def use(h, j):
         lanes = sumsq.shape[1]
         squares = sumsq[...]
@@ -489,7 +505,7 @@
         a = axes[h][0]
         return send(
             ring_s.at[h, d, m],
-            ring_r.at[h, d, m + 2],
+            ring_r.at[h, d, m + pieces],
             ring_ss.at[h, d, m],
             ring_rs.at[h, d, m],
             a,
@@ -497,24 +513,26 @@
         )
 
     def ring_step(m, carry):
-        away = lax.div(n - m, 2)
+        group = lax.div(m, per)
+        within = lax.rem(m, per)
+        away = lax.div(n - group, 2)
+        odd = lax.rem(group, 2)
         for h in (0, 1):
             for d in (0, 1):
-                odd = lax.rem(m, 2)
-                s = odd if d == 0 else 1 - odd
+                s = (odd if d == 0 else 1 - odd) * per + within
                 shift = n - away if d else away
                 j = lax.rem(pos[axes[h][0]] + shift, n)
                 value = down(h, j, s)
 
-                @pl.when(m >= 2)
+                @pl.when(m >= pieces)
                 def _():
-                    ring_copy(h, d, m - 2).wait_recv()
+                    ring_copy(h, d, m - pieces).wait_recv()
 
                 ring_s[h, d, m] = (value + ring_r[h, d, m].astype(F32)).astype(BF16)
                 ring_copy(h, d, m).start()
         return carry
 
-    lax.fori_loop(0, n - 1, ring_step, 0)
+    lax.fori_loop(0, messages, ring_step, 0)
 
     def two_copy(h, r):
         b = axes[h][1]
@@ -523,16 +541,17 @@
         )
 
     for h in (0, 1):
-        for s in (0, 1):
+        for s in range(pieces):
             down_sum[h, :, pl.ds(s * wide, wide)] = down(h, pos[axes[h][0]], s)
     for h in (0, 1):
         for d in (0, 1):
-            for m in (n - 3, n - 2):
+            for m in range(messages - pieces, messages):
                 ring_copy(h, d, m).wait_recv()
-        for s in (0, 1):
+        for s in range(pieces):
             some = pl.ds(s * wide, wide)
-            plus = ring_r[h, 0, n - s].astype(F32)
-            minus = ring_r[h, 1, n - 1 + s].astype(F32)
+            late = messages + per + s % per
+            plus = ring_r[h, 0, late - s // per * per].astype(F32)
+            minus = ring_r[h, 1, late - per + s // per * per].astype(F32)
             down_sum[h, :, some] = down_sum[h, :, some] + plus + minus
         for j in range(n):
             two_s[h, j] = down_sum[h, pl.ds(j * rows, rows), :].astype(BF16)
@@ -556,7 +575,9 @@
 
     for h in (0, 1):
         a, b = axes[h]
-        all_but_one(heads_all.at[h, seen_w, :], heads_ss.at[h], heads_rs.at[h], a).wait_send()
+        for d in (0, 1):
+            for k in range(reach):
+                heads_copy(h, d, k).wait_send()
         all_but_one(strm.at[h, pl.ds(0, n - 1)], strm_ss.at[h], strm_rs.at[h], a).wait_send()
         for c in range(chunks):
             all_but_one(
@@ -574,7 +595,7 @@
             for k in range(reach):
                 for c in range(chunks):
                     agb_copy(h, d, k, c, behind(h, d, k), k < reach - 1).wait_send()
-            for m in range(n - 1):
+            for m in range(messages):
                 ring_copy(h, d, m).wait_send()
     for copy in last:
         copy.wait()
@@ -607,6 +628,8 @@
     slots = -(-(hidden + k_out) // 128) * 128
     strip = width // 2 // n
     chunks = 2
+    pieces = 4
+    messages = pieces // 2 * (n - 1)
     chunk = strip // chunks
     block = tokens // n
     reach = n // 2
@@ -646,8 +669,8 @@
         pltpu.VMEM((tokens, 128), F32),
         pltpu.VMEM((2, tokens, slots), BF16),
         pltpu.VMEM((2, tokens, 128), BF16),
-        pltpu.VMEM((2, 2, n - 1, block, width // 4), BF16),
-        pltpu.VMEM((2, 2, n + 1, block, width // 4), BF16),
+        pltpu.VMEM((2, 2, messages, block, width // 2 // pieces), BF16),
+        pltpu.VMEM((2, 2, messages + pieces, block, width // 2 // pieces), BF16),
         pltpu.VMEM((2, n, rows, width // 2), BF16),
         pltpu.VMEM((2, n - 1, rows, width // 2), BF16),
         pltpu.VMEM((2, n, rows, strip), F32),
@@ -656,11 +679,11 @@
         pltpu.VMEM((rows, width), BF16),
         dma((4 + 2 * chunks + 14,)),
     ]
-    scratch += [dma((2,)), dma((2,)), dma((2, chunks)), dma((2, chunks))]
+    scratch += [dma((2, 2, reach)), dma((2, 2, reach)), dma((2, chunks)), dma((2, chunks))]
     scratch += [dma((2, chunks, cores)), dma((2, chunks, cores)), dma((2,)), dma((2,))]
     scratch += [dma((2, chunks)) for _ in range(4)]
     scratch += [dma((2, 2, reach, chunks)), dma((2, 2, reach, chunks))]
-    scratch += [dma((2, 2, n - 1)), dma((2, 2, n - 1))]
+    scratch += [dma((2, 2, messages)), dma((2, 2, messages))]
     scratch += [dma((2,)) for _ in range(4)]
     return pl.pallas_call(
         functools.partial(kernel, n, cores),

time: 104 us -> 108 us (1.038)
  Pallas kernels: 102 us -> 106 us
    pallas_call x1, Pallas kernels: 102 us -> 106 us  [local(): pl.pallas_call(functools.partial(kernel, n, cores), out_shape=jax.ShapeDt...]
where the time goes in v5:
time: 108 us; the launch traced here: 107 us
  Pallas kernels  106 us (98%)
  local copies, waits for them, and re-layouts  1.49 us (1%)
    pallas_call x1, Pallas kernels, local(): pl.pallas_call(functools.partial(kernel, n, cores), out_shape=jax.ShapeDt...  106 us

profile of v5, /device:TPU:514, one launch (start us, length us, event | category | flops | bytes accessed | tf_op | source)
XLA Modules:
  0.0 107.1 jit_solution(9519065700187546945)
XLA Ops:
  0.0 105.6 %shard_map.163 = bf16[4,8192]{1,0:T(4,128)(2,1)} custom-call(bf16[64,256]{1,0:T(8,128)(2,1)} %bitcast.15, bf16[4,8192]{1,0:T(4,128)(2,1)} %stream_ref.1, bf16[64,8192]{1,0:T(8,128)(2,1)} %projw_ref.1, f32[1,8192]{1,0:T(1,128)} %bitcast.16, f32[1,8192]{1,0:T(1,128)} %bitcast.17, bf16[224,8192]{1,0:T(8,128)(2,1)} %bitcast.11, f32[1,224]{1,0:T(1,128)} %bitcast.20, ...), custom_call_target="tpu_custom_call" | custom-call | tf_op jit(solution)/shard_map/pallas_call | solution.py:688
  105.6 1.5 %copy.19 = bf16[4,8192]{1,0:T(4,128)(2,1)} copy(bf16[4,8192]{1,0:T(4,128)(2,1)} %shard_map.163) | data formatting | bytes 131072

commit v6 on v4

--- a/solution.py
+++ b/solution.py
@@ -121,7 +121,10 @@
     strip = half // n
     block = tokens // n
     sub = tokens // 2
-    wide = half // 2
+    wide = ring_s.shape[4]
+    pieces = half // wide
+    per = pieces // 2
+    messages = per * (n - 1)
     reach = n // 2
     axes = (("tensor_0", "tensor_1"), ("tensor_1", "tensor_0"))
     pos = {name: lax.axis_index(name) for name in TENSOR}
@@ -187,14 +190,14 @@
     def heads_copy(h, r):
         a = axes[h][0]
         there = heads_all.at[h, place(pos[a]), :]
-        return send(there, there, heads_ss.at[h], heads_rs.at[h], a, at(a, r))
+        return send(there, there, heads_ss.at[0], heads_rs.at[h], a, at(a, r))
 
     def w_copy(h, c, r):
         a = axes[h][0]
         return send(
             projw_ref.at[:, own_part(h, at(a, r), c)],
             w_all.at[h, c, place(pos[a]), mine],
-            w_ss.at[h, c],
+            w_ss.at[0],
             w_rs.at[h, c],
             a,
             at(a, r),
@@ -203,14 +206,14 @@
     def share_copy(h, c, q):
         there = w_all.at[h, c, :, mine]
         to = lax.rem(core + q, cores)
-        return send(there, there, share_ss.at[h, c, q], share_rs.at[h, c, q], "seq", to)
+        return send(there, there, share_ss.at[q - 1], share_rs.at[h, c, q - 1], "seq", to)
 
     def strm_copy(h, r):
         a = axes[h][0]
         return send(
             stream_ref.at[:, cols(h, at(a, r))],
             strm.at[h, pos[a]],
-            strm_ss.at[h],
+            strm_ss.at[0],
             strm_rs.at[h],
             a,
             at(a, r),
@@ -301,7 +304,7 @@
     sumsq[...] = jnp.zeros_like(sumsq)
     for h in (0, 1):
         for d in (0, 1):
-            for m in (0, 1):
+            for m in range(pieces):
                 ring_r[h, d, m] = jnp.zeros((block, wide), BF16)
 
     def one_copy(h, c, r):
@@ -310,7 +313,7 @@
         return send(
             t_half.at[h, c, away, :],
             r_one.at[h, c, r - 1],
-            one_ss.at[h, c],
+            one_ss.at[0],
             one_rs.at[h, c],
             b,
             at(b, r),
@@ -323,7 +326,7 @@
             a = axes[h][0]
             first[each * h + 2 + c].wait()
             all_but_one(
-                w_all.at[h, c, seen_w, mine], w_ss.at[h, c], w_rs.at[h, c], a
+                w_all.at[h, c, seen_w, mine], w_ss.at[0], w_rs.at[h, c], a
             ).wait_recv()
             for q in range(1, cores):
                 share_copy(h, c, q).start()
@@ -331,7 +334,7 @@
             a = axes[h][0]
             if c == 0:
                 all_but_one(
-                    heads_all.at[h, seen_w, :], heads_ss.at[h], heads_rs.at[h], a
+                    heads_all.at[h, seen_w, :], heads_ss.at[0], heads_rs.at[h], a
                 ).wait_recv()
                 if h == 0:
                     turn = perm[...]
@@ -349,12 +352,12 @@
         a, b = axes[h]
         own = pl.ds(pl.multiple_of(pos[b] * block, block), block)
         there = y_all.at[h, pos[a], c, own, :]
-        return send(there, there, aga_ss.at[h, c], aga_rs.at[h, c], b, at(b, r))
+        return send(there, there, aga_ss.at[0], aga_rs.at[h, c], b, at(b, r))
 
     def mix_copy(h, r):
         a = axes[h][0]
         there = mix_r.at[h, :, pl.ds(pl.multiple_of(pos[a] * strip, strip), strip)]
-        return send(mix_s.at[h, at(a, r)], there, mix_ss.at[h], mix_rs.at[h], a, at(a, r))
+        return send(mix_s.at[h, at(a, r)], there, mix_ss.at[0], mix_rs.at[h], a, at(a, r))
 
     for c in range(chunks):
         for h in (0, 1):
@@ -366,9 +369,9 @@
             if c == 0:
                 first[each * h + 1].wait()
                 all_but_one(
-                    strm.at[h, pl.ds(0, n - 1)], strm_ss.at[h], strm_rs.at[h], a
+                    strm.at[h, pl.ds(0, n - 1)], strm_ss.at[0], strm_rs.at[h], a
                 ).wait_recv()
-            all_but_one(r_one.at[h, c], one_ss.at[h, c], one_rs.at[h, c], b).wait_recv()
+            all_but_one(r_one.at[h, c], one_ss.at[0], one_rs.at[h, c], b).wait_recv()
             for r in range(1, n):
                 total += r_one[h, c, r - 1].astype(F32)
             mixed[h, c] = total * pscale_ref[:, here]
@@ -380,18 +383,12 @@
                 aga_copy(h, c, r).start()
             for j in range(n):
                 mix_s[h, j, :, within] = mixed[h, c, pl.ds(j * rows, rows), :]
-    for h in (0, 1):
-        me = pos[axes[h][0]]
-        for r in offsets:
-            mix_copy(h, r).start()
-        mix_r[h, :, pl.ds(pl.multiple_of(me * strip, strip), strip)] = mix_s[h, me]
-
     def agb_copy(h, d, k, c, strip_id, whole):
         a = axes[h][0]
         some = pl.ds(0, tokens) if whole else pl.ds(d * sub, sub)
         there = y_all.at[h, strip_id, c, some, :]
         return send(
-            there, there, agb_ss.at[h, d, k, c], agb_rs.at[h, d, k, c], a, at(a, 1 - 2 * d)
+            there, there, agb_ss.at[0], agb_rs.at[h, d, k, c], a, at(a, 1 - 2 * d)
         )
 
     def behind(h, d, k):
@@ -419,7 +416,7 @@
         for h in (0, 1):
             a, b = axes[h]
             all_but_one(
-                y_all.at[h, 0, c, seen_b, :], aga_ss.at[h, c], aga_rs.at[h, c], b
+                y_all.at[h, 0, c, seen_b, :], aga_ss.at[0], aga_rs.at[h, c], b
             ).wait_recv()
             for d in (0, 1):
                 agb_copy(h, d, 0, c, pos[a], True).start()
@@ -450,6 +447,11 @@
 
     lax.fori_loop(1, reach, gather_step, 0)
     for h in (0, 1):
+        me = pos[axes[h][0]]
+        for r in offsets:
+            mix_copy(h, r).start()
+        mix_r[h, :, pl.ds(pl.multiple_of(me * strip, strip), strip)] = mix_s[h, me]
+    for h in (0, 1):
         j = behind(h, 0, reach)
         for d in (0, 1):
             for c in range(chunks):
@@ -489,93 +491,102 @@
         a = axes[h][0]
         return send(
             ring_s.at[h, d, m],
-            ring_r.at[h, d, m + 2],
-            ring_ss.at[h, d, m],
+            ring_r.at[h, d, m + pieces],
+            ring_ss.at[0],
             ring_rs.at[h, d, m],
             a,
             at(a, 1 - 2 * d),
         )
 
     def ring_step(m, carry):
-        away = lax.div(n - m, 2)
+        group = lax.div(m, per)
+        within = lax.rem(m, per)
+        away = lax.div(n - group, 2)
+        odd = lax.rem(group, 2)
         for h in (0, 1):
             for d in (0, 1):
-                odd = lax.rem(m, 2)
-                s = odd if d == 0 else 1 - odd
+                s = (odd if d == 0 else 1 - odd) * per + within
                 shift = n - away if d else away
                 j = lax.rem(pos[axes[h][0]] + shift, n)
                 value = down(h, j, s)
 
-                @pl.when(m >= 2)
+                @pl.when(m >= pieces)
                 def _():
-                    ring_copy(h, d, m - 2).wait_recv()
+                    ring_copy(h, d, m - pieces).wait_recv()
 
                 ring_s[h, d, m] = (value + ring_r[h, d, m].astype(F32)).astype(BF16)
                 ring_copy(h, d, m).start()
         return carry
 
-    lax.fori_loop(0, n - 1, ring_step, 0)
-
-    def two_copy(h, r):
+    lax.fori_loop(0, messages, ring_step, 0)
+
+    def two_copy(h, p, r):
         b = axes[h][1]
         return send(
-            two_s.at[h, at(b, r)], r_two.at[h, r - 1], two_ss.at[h], two_rs.at[h], b, at(b, r)
-        )
-
-    for h in (0, 1):
-        for s in (0, 1):
-            down_sum[h, :, pl.ds(s * wide, wide)] = down(h, pos[axes[h][0]], s)
-    for h in (0, 1):
-        for d in (0, 1):
-            for m in (n - 3, n - 2):
-                ring_copy(h, d, m).wait_recv()
-        for s in (0, 1):
-            some = pl.ds(s * wide, wide)
-            plus = ring_r[h, 0, n - s].astype(F32)
-            minus = ring_r[h, 1, n - 1 + s].astype(F32)
-            down_sum[h, :, some] = down_sum[h, :, some] + plus + minus
-        for j in range(n):
-            two_s[h, j] = down_sum[h, pl.ds(j * rows, rows), :].astype(BF16)
-        for r in offsets:
-            two_copy(h, r).start()
+            two_s.at[h, p, at(b, r)],
+            r_two.at[h, p, r - 1],
+            two_ss.at[0],
+            two_rs.at[h, p],
+            b,
+            at(b, r),
+        )
+
+    for h in (0, 1):
+        for s in range(pieces):
+            down_sum[h, s] = down(h, pos[axes[h][0]], s)
+    for p in range(per):
+        for h in (0, 1):
+            for d in (0, 1):
+                for m in (messages - pieces + p, messages - per + p):
+                    ring_copy(h, d, m).wait_recv()
+            for q in (0, 1):
+                s = q * per + p
+                plus = ring_r[h, 0, messages + (1 - q) * per + p].astype(F32)
+                minus = ring_r[h, 1, messages + q * per + p].astype(F32)
+                down_sum[h, s] = down_sum[h, s] + plus + minus
+                for j in range(n):
+                    few = down_sum[h, s, pl.ds(j * rows, rows), :]
+                    two_s[h, p, j, :, pl.ds(q * wide, wide)] = few.astype(BF16)
+            for r in offsets:
+                two_copy(h, p, r).start()
 
     last = []
     for h in (0, 1):
-        a, b = axes[h]
-        all_but_one(mix_s.at[h, pl.ds(0, n - 1)], mix_ss.at[h], mix_rs.at[h], a).wait_recv()
-        total = mix_r[h] + two_s[h, pos[b]].astype(F32)
-        all_but_one(r_two.at[h], two_ss.at[h], two_rs.at[h], b).wait_recv()
-        for r in range(1, n):
-            total += r_two[h, r - 1].astype(F32)
+        a = axes[h][0]
+        all_but_one(mix_s.at[h, pl.ds(0, n - 1)], mix_ss.at[0], mix_rs.at[h], a).wait_recv()
+    for p in range(per):
+        for h in (0, 1):
+            b = axes[h][1]
+            total = two_s[h, p, pos[b]].astype(F32)
+            all_but_one(r_two.at[h, p], two_ss.at[0], two_rs.at[h, p], b).wait_recv()
+            for r in range(1, n):
+                total += r_two[h, p, r - 1].astype(F32)
+            for q in (0, 1):
+                here = (q * per + p) * wide
+                value = total[:, q * wide : (q + 1) * wide] + mix_r[h, :, pl.ds(here, wide)]
+                out_v[:, pl.ds(h * half + here, wide)] = value.astype(BF16)
+    for h in (0, 1):
         here = pl.ds(h * half, half)
-        out_v[:, here] = total.astype(BF16)
         last.append(
             pltpu.make_async_copy(out_v.at[:, here], out_ref.at[:, here], load_sem.at[3 * h])
         )
         last[h].start()
 
-    for h in (0, 1):
-        a, b = axes[h]
-        all_but_one(heads_all.at[h, seen_w, :], heads_ss.at[h], heads_rs.at[h], a).wait_send()
-        all_but_one(strm.at[h, pl.ds(0, n - 1)], strm_ss.at[h], strm_rs.at[h], a).wait_send()
-        for c in range(chunks):
-            all_but_one(
-                w_all.at[h, c, seen_w, mine], w_ss.at[h, c], w_rs.at[h, c], a
-            ).wait_send()
-            for q in range(1, cores):
-                share_copy(h, c, q).wait_send()
-            all_but_one(
-                y_all.at[h, 0, c, seen_b, :], aga_ss.at[h, c], aga_rs.at[h, c], b
-            ).wait_send()
-            all_but_one(r_one.at[h, c], one_ss.at[h, c], one_rs.at[h, c], b).wait_send()
-        all_but_one(mix_s.at[h, pl.ds(0, n - 1)], mix_ss.at[h], mix_rs.at[h], a).wait_send()
-        all_but_one(r_two.at[h], two_ss.at[h], two_rs.at[h], b).wait_send()
-        for d in (0, 1):
-            for k in range(reach):
-                for c in range(chunks):
-                    agb_copy(h, d, k, c, behind(h, d, k), k < reach - 1).wait_send()
-            for m in range(n - 1):
-                ring_copy(h, d, m).wait_send()
+    def all_sent(ref, ssem, rsem):
+        send(ref, ref, ssem, rsem, TENSOR[0], at(TENSOR[0], 1)).wait_send()
+
+    most = pl.ds(0, n - 1)
+    all_sent(heads_all.at[:, seen_w, :], heads_ss.at[0], heads_rs.at[0])
+    all_sent(w_all.at[:, :, seen_w, mine], w_ss.at[0], w_rs.at[0, 0])
+    for q in range(1, cores):
+        all_sent(w_all.at[:, :, :, mine], share_ss.at[q - 1], share_rs.at[0, 0, q - 1])
+    all_sent(strm.at[:, most], strm_ss.at[0], strm_rs.at[0])
+    all_sent(r_one, one_ss.at[0], one_rs.at[0, 0])
+    all_sent(y_all.at[:, 0, :, seen_b, :], aga_ss.at[0], aga_rs.at[0, 0])
+    all_sent(y_all.at[:, most], agb_ss.at[0], agb_rs.at[0, 0, 0, 0])
+    all_sent(mix_s.at[:, most], mix_ss.at[0], mix_rs.at[0])
+    all_sent(ring_s, ring_ss.at[0], ring_rs.at[0, 0, 0])
+    all_sent(r_two, two_ss.at[0], two_rs.at[0, 0])
     for copy in last:
         copy.wait()
 
@@ -607,6 +618,8 @@
     slots = -(-(hidden + k_out) // 128) * 128
     strip = width // 2 // n
     chunks = 2
+    pieces = 4
+    messages = pieces // 2 * (n - 1)
     chunk = strip // chunks
     block = tokens // n
     reach = n // 2
@@ -646,22 +659,29 @@
         pltpu.VMEM((tokens, 128), F32),
         pltpu.VMEM((2, tokens, slots), BF16),
         pltpu.VMEM((2, tokens, 128), BF16),
-        pltpu.VMEM((2, 2, n - 1, block, width // 4), BF16),
-        pltpu.VMEM((2, 2, n + 1, block, width // 4), BF16),
-        pltpu.VMEM((2, n, rows, width // 2), BF16),
-        pltpu.VMEM((2, n - 1, rows, width // 2), BF16),
+        pltpu.VMEM((2, 2, messages, block, width // 2 // pieces), BF16),
+        pltpu.VMEM((2, 2, messages + pieces, block, width // 2 // pieces), BF16),
+        pltpu.VMEM((2, pieces // 2, n, rows, width // pieces), BF16),
+        pltpu.VMEM((2, pieces // 2, n - 1, rows, width // pieces), BF16),
         pltpu.VMEM((2, n, rows, strip), F32),
         pltpu.VMEM((2, rows, width // 2), F32),
-        pltpu.VMEM((2, block, width // 2), F32),
+        pltpu.VMEM((2, pieces, block, width // 2 // pieces), F32),
         pltpu.VMEM((rows, width), BF16),
         dma((4 + 2 * chunks + 14,)),
     ]
-    scratch += [dma((2,)), dma((2,)), dma((2, chunks)), dma((2, chunks))]
-    scratch += [dma((2, chunks, cores)), dma((2, chunks, cores)), dma((2,)), dma((2,))]
-    scratch += [dma((2, chunks)) for _ in range(4)]
-    scratch += [dma((2, 2, reach, chunks)), dma((2, 2, reach, chunks))]
-    scratch += [dma((2, 2, n - 1)), dma((2, 2, n - 1))]
-    scratch += [dma((2,)) for _ in range(4)]
+    for sends, receives in (
+        (1, (2,)),
+        (1, (2, chunks)),
+        (cores, (2, chunks, cores)),
+        (1, (2,)),
+        (1, (2, chunks)),
+        (1, (2, chunks)),
+        (1, (2, 2, reach, chunks)),
+        (1, (2, 2, messages)),
+        (1, (2, pieces // 2)),
+        (1, (2,)),
+    ):
+        scratch += [dma((sends,)), dma(receives)]
     return pl.pallas_call(
         functools.partial(kernel, n, cores),
         out_shape=jax.ShapeDtypeStruct((rows, width), BF16),

time: 104 us -> 100 us (0.962)
  Pallas kernels: 102 us -> 98.7 us
    pallas_call x1, Pallas kernels: 102 us -> 98.7 us  [local(): pl.pallas_call(functools.partial(kernel, n, cores), out_shape=jax.ShapeDt...]
where the time goes in v6:
time: 100 us
  Pallas kernels  98.7 us (99%)
  local copies, waits for them, and re-layouts  1.49 us (1%)
    pallas_call x1, Pallas kernels, local(): pl.pallas_call(functools.partial(kernel, n, cores), out_shape=jax.ShapeDt...  98.7 us

profile of v6, /device:TPU:514, one launch (start us, length us, event | category | flops | bytes accessed | tf_op | source)
XLA Modules:
  0.0 100.2 jit_solution(6593964634004435232)
XLA Ops:
  0.0 98.7 %shard_map.163 = bf16[4,8192]{1,0:T(4,128)(2,1)} custom-call(bf16[64,256]{1,0:T(8,128)(2,1)} %bitcast.15, bf16[4,8192]{1,0:T(4,128)(2,1)} %stream_ref.1, bf16[64,8192]{1,0:T(8,128)(2,1)} %projw_ref.1, f32[1,8192]{1,0:T(1,128)} %bitcast.16, f32[1,8192]{1,0:T(1,128)} %bitcast.17, bf16[224,8192]{1,0:T(8,128)(2,1)} %bitcast.11, f32[1,224]{1,0:T(1,128)} %bitcast.20, ...), custom_call_target="tpu_custom_call" | custom-call | tf_op jit(solution)/shard_map/pallas_call | solution.py:685
  98.7 1.5 %copy.19 = bf16[4,8192]{1,0:T(4,128)(2,1)} copy(bf16[4,8192]{1,0:T(4,128)(2,1)} %shard_map.163) | data formatting | bytes 131072

commit v7 on v6

--- a/solution.py
+++ b/solution.py
@@ -85,7 +85,6 @@
     mix_s,
     mix_r,
     down_sum,
-    out_v,
     load_sem,
     heads_ss,
     heads_rs,
@@ -550,7 +549,6 @@
             for r in offsets:
                 two_copy(h, p, r).start()
 
-    last = []
     for h in (0, 1):
         a = axes[h][0]
         all_but_one(mix_s.at[h, pl.ds(0, n - 1)], mix_ss.at[0], mix_rs.at[h], a).wait_recv()
@@ -564,14 +562,7 @@
             for q in (0, 1):
                 here = (q * per + p) * wide
                 value = total[:, q * wide : (q + 1) * wide] + mix_r[h, :, pl.ds(here, wide)]
-                out_v[:, pl.ds(h * half + here, wide)] = value.astype(BF16)
-    for h in (0, 1):
-        here = pl.ds(h * half, half)
-        last.append(
-            pltpu.make_async_copy(out_v.at[:, here], out_ref.at[:, here], load_sem.at[3 * h])
-        )
-        last[h].start()
-
+                out_ref[:, pl.ds(h * half + here, wide)] = value.astype(BF16)
     def all_sent(ref, ssem, rsem):
         send(ref, ref, ssem, rsem, TENSOR[0], at(TENSOR[0], 1)).wait_send()
 
@@ -587,9 +578,6 @@
     all_sent(mix_s.at[:, most], mix_ss.at[0], mix_rs.at[0])
     all_sent(ring_s, ring_ss.at[0], ring_rs.at[0, 0, 0])
     all_sent(r_two, two_ss.at[0], two_rs.at[0, 0])
-    for copy in last:
-        copy.wait()
-
 
 def local(n, cores, *args):
     (
@@ -624,7 +612,7 @@
     block = tokens // n
     reach = n // 2
     index = pltpu.SMEM(gate_index.shape, jnp.int32)
-    hbm = pl.BlockSpec(memory_space=pl.ANY)
+    hbm = pl.BlockSpec(memory_space=pltpu.HBM)
     dma = pltpu.SemaphoreType.DMA
     scratch = [
         pltpu.VMEM((1, width), F32),
@@ -666,13 +654,12 @@
         pltpu.VMEM((2, n, rows, strip), F32),
         pltpu.VMEM((2, rows, width // 2), F32),
         pltpu.VMEM((2, pieces, block, width // 2 // pieces), F32),
-        pltpu.VMEM((rows, width), BF16),
         dma((4 + 2 * chunks + 14,)),
     ]
     for sends, receives in (
         (1, (2,)),
         (1, (2, chunks)),
-        (cores, (2, chunks, cores)),
+        (cores, (2, chunks, max(cores - 1, 1))),
         (1, (2,)),
         (1, (2, chunks)),
         (1, (2, chunks)),
@@ -686,29 +673,34 @@
         functools.partial(kernel, n, cores),
         out_shape=jax.ShapeDtypeStruct((rows, width), BF16),
         in_specs=[hbm] * len(args),
-        out_specs=hbm,
+        out_specs=pl.BlockSpec(memory_space=pltpu.VMEM),
         scratch_shapes=scratch,
         compiler_params=pltpu.CompilerParams(
-            collective_id=0, has_side_effects=True, vmem_limit_bytes=60 * 1024 * 1024
+            collective_id=0, has_side_effects=True, vmem_limit_bytes=48 * 1024 * 1024
         ),
     )(
-        heads_out.T,
-        stream_in,
-        proj_levels,
-        proj_scale[None, :],
-        norm_gain[None, :],
-        gate_levels.T,
-        gate_scale[None, :],
-        gate_index,
-        gate_extra.T,
-        up_levels.T,
-        up_scale[None, :],
-        up_index,
-        up_extra.T,
-        down_levels,
-        down_scale[None, :],
-        down_index,
-        down_extra.T,
+        *(
+            pltpu.with_memory_space_constraint(arg, pltpu.HBM)
+            for arg in (
+                heads_out.T,
+                stream_in,
+                proj_levels,
+                proj_scale[None, :],
+                norm_gain[None, :],
+                gate_levels.T,
+                gate_scale[None, :],
+                gate_index,
+                gate_extra.T,
+                up_levels.T,
+                up_scale[None, :],
+                up_index,
+                up_extra.T,
+                down_levels,
+                down_scale[None, :],
+                down_index,
+                down_extra.T,
+            )
+        )
     )
 
 

time: 100 us -> 98.9 us (0.989)
  no operation moved by 1% of the time
where the time goes in v7:
time: 98.9 us; the launch traced here: 98.7 us
  Pallas kernels  98.1 us (99%)
    pallas_call x1, Pallas kernels, local(): pl.pallas_call(functools.partial(kernel, n, cores), out_shape=jax.ShapeDt...  98.1 us

profile of v7, /device:TPU:514, one launch (start us, length us, event | category | flops | bytes accessed | tf_op | source)
XLA Modules:
  0.0 98.7 jit_solution(11949242867012897931)
XLA Ops:
  0.0 98.1 %shard_map.163 = bf16[4,8192]{1,0:T(4,128)(2,1)S(1)} custom-call(bf16[64,256]{1,0:T(8,128)(2,1)} %bitcast.15, bf16[4,8192]{1,0:T(4,128)(2,1)} %stream_ref.1, bf16[64,8192]{1,0:T(8,128)(2,1)} %projw_ref.1, f32[1,8192]{1,0:T(1,128)} %bitcast.16, f32[1,8192]{1,0:T(1,128)} %bitcast.17, bf16[224,8192]{1,0:T(8,128)(2,1)} %bitcast.11, f32[1,224]{1,0:T(1,128)} %bitcast.20, ...), custom_call_target="tpu_custom_call" | custom-call | tf_op jit(solution)/shard_map/pallas_call | solution.py:672
  98.1 0.6 copy.19

commit v8 on v7

--- a/solution.py
+++ b/solution.py
@@ -460,11 +460,16 @@
     mean_sq = jnp.sum(sumsq[...], axis=1, keepdims=True) * (1.0 / width)
     factor = lax.rsqrt(mean_sq + 1e-05)
 
+    upper = hidden // 128 * 128
+
     def branch(base, scale_ref, pick):
         part = acc[:, pl.ds(base, slots)]
         scale = jnp.concatenate([scale_ref[...], jnp.zeros((1, slots - hidden), F32)], axis=1)
         added = jnp.dot(
-            part, pick[...], precision=lax.Precision.HIGHEST, preferred_element_type=F32
+            part[:, upper:],
+            pick[pl.ds(upper, slots - upper), :],
+            precision=lax.Precision.HIGHEST,
+            preferred_element_type=F32,
         )
         return (part * scale + added) * factor
 

time: 98.9 us -> 98.8 us (level)
  no operation moved by 1% of the time
where the time goes in v8:
time: 98.8 us; the launch traced here: 98.7 us
  Pallas kernels  98 us (99%)
    pallas_call x1, Pallas kernels, local(): pl.pallas_call(functools.partial(kernel, n, cores), out_shape=jax.ShapeDt...  98 us

profile of v8, /device:TPU:514, one launch (start us, length us, event | category | flops | bytes accessed | tf_op | source)
XLA Modules:
  0.0 98.7 jit_solution(3663667117397328255)
XLA Ops:
  0.0 98.0 %shard_map.163 = bf16[4,8192]{1,0:T(4,128)(2,1)S(1)} custom-call(bf16[64,256]{1,0:T(8,128)(2,1)} %bitcast.15, bf16[4,8192]{1,0:T(4,128)(2,1)} %stream_ref.1, bf16[64,8192]{1,0:T(8,128)(2,1)} %projw_ref.1, f32[1,8192]{1,0:T(1,128)} %bitcast.16, f32[1,8192]{1,0:T(1,128)} %bitcast.17, bf16[224,8192]{1,0:T(8,128)(2,1)} %bitcast.11, f32[1,224]{1,0:T(1,128)} %bitcast.20, ...), custom_call_target="tpu_custom_call" | custom-call | tf_op jit(solution)/shard_map/pallas_call | solution.py:677
  98.0 0.6 copy.19
